TPU v7x, 128 devices: a whole 4x4x4 slice. The times are simulated.
128 devices in a mesh: dp: 32 (over z, x, core), tensor: 4 (over y).
Axes of the slice: x: 4, y: 4, z: 4, core: 2. Of those that a mesh axis runs over, the one named last changes fastest.
Arguments:
- activations: bfloat16 [64, 128, 4096], P('dp'), may hold values from -6 to 6
- out_grads: bfloat16 [64, 128, 20480], P('dp', None, 'tensor'), may hold values from -0.625 to 0.625
- act_scale: bfloat16 [64, 32], P('dp'), may hold values from 1 to 16
- grad_scale: bfloat16 [64, 1, 20480], P('dp', None, 'tensor'), may hold values from 1 to 72
- moment: float32 [20480, 4096], P(('tensor', 'dp')), may hold values from -0.6 to 0.6
- second: float32 [20480, 4096], P(('tensor', 'dp')), may hold values from 0.1 to 1
- master: float32 [20480, 4096], P(('tensor', 'dp')), may hold values from -0.0625 to 0.0625
Outputs:
- new_moment: float32 [20480, 4096], P(('tensor', 'dp'))
- new_second: float32 [20480, 4096], P(('tensor', 'dp'))
- new_master: float32 [20480, 4096], P(('tensor', 'dp'))
- weights: bfloat16 [20480, 4096], P(('tensor', 'dp'))
All inputs are finite; a program needn't handle non-finite values.
Results may differ from a plain program's by a relative error of at most 0.015.
Values may be sent and summed in bfloat16 or wider, within the bound.
A program may use at most 192 MiB of HBM per device.

v0:
```python
import functools

import jax
import jax.numpy as jnp
from jax import lax
from jax.sharding import Mesh
from jax.sharding import PartitionSpec as P

FF = 20480
ROWS = 4096
TILE = 128
DP = ("dp_0", "dp_1", "dp_2")
DP_TENSOR = ("dp_0", "dp_1", "dp_2", "tensor")
TENSOR_DP = ("tensor", "dp_0", "dp_1", "dp_2")


clip_rms = 1.0
beta_first = 0.9
beta_second = 0.95
learn_rate = 0.003
adam_eps = 1e-08


def over_axes(shard, axes):
    return functools.reduce(lax.psum, axes, shard)


def widen(act_scale):
    tiles = act_scale.astype(jnp.float32)
    spread = jnp.broadcast_to(tiles[:, :, None], tiles.shape + (TILE,))
    return spread.reshape(tiles.shape[0], tiles.shape[1] * TILE)


def transposed_product(grads_rows, acts_rows):
    return lax.dot_general(
        grads_rows, acts_rows, (((0,), (0,)), ((), ())), preferred_element_type=jnp.float32
    )


def per_device(activations, out_grads, act_scale, grad_scale, moment, second, master):
    weight_rows = activations.shape[2]
    local_tokens = activations.shape[0] * activations.shape[1]
    acts_deq = (
        (activations.astype(jnp.float32) * widen(act_scale)[:, None, :])
        .astype(jnp.bfloat16)
        .reshape(local_tokens, weight_rows)
    )
    grads_deq = (
        (out_grads.astype(jnp.float32) * grad_scale.astype(jnp.float32))
        .astype(jnp.bfloat16)
        .reshape(local_tokens, out_grads.shape[2])
    )
    grad_owned = lax.psum_scatter(
        transposed_product(grads_deq, acts_deq).astype(jnp.bfloat16),
        DP,
        scatter_dimension=0,
        tiled=True,
    ).astype(jnp.float32)
    squares = over_axes(jnp.sum(grad_owned * grad_owned), DP_TENSOR)
    limit = clip_rms * jnp.sqrt(jnp.float32(FF * ROWS))
    factor = jnp.minimum(1.0, limit / jnp.sqrt(squares))
    clipped = factor * grad_owned
    new_moment = beta_first * moment + (1.0 - beta_first) * clipped
    new_second = beta_second * second + (1.0 - beta_second) * clipped * clipped
    new_master = master - learn_rate * new_moment / (jnp.sqrt(new_second) + adam_eps)
    weights = new_master.astype(jnp.bfloat16)
    return (new_moment, new_second, new_master, weights)


def solution(mesh):
    finer = Mesh(
        mesh.devices.reshape(4, 4, 2, mesh.shape["tensor"]), ("dp_0", "dp_1", "dp_2", "tensor")
    )
    in_specs = (
        P(DP, None, None),
        P(DP, None, "tensor"),
        P(DP, None),
        P(DP, None, "tensor"),
        P(TENSOR_DP, None),
        P(TENSOR_DP, None),
        P(TENSOR_DP, None),
    )
    out_specs = (P(TENSOR_DP, None), P(TENSOR_DP, None), P(TENSOR_DP, None), P(TENSOR_DP, None))
    return jax.shard_map(
        per_device, mesh=finer, in_specs=in_specs, out_specs=out_specs, check_vma=False
    )
```

profile of v0, /device:TPU:0, one launch (start us, length us, event | category | flops | bytes accessed | tf_op | source)
XLA Modules:
  0.0 274.4 jit_solution(12825549376815564013)
XLA Ops:
  7.2 0.0 reduce-scatter.2.cloned.1.call-start
  7.2 0.7 convert_element_type.28
  7.9 0.1 broadcast_bitcast_fusion
  8.0 0.7 bitcast_convert_fusion.1
  8.7 18.6 %bitcast_convert_fusion = bf16[5120,4096]{1,0:T(8,128)(2,1)} fusion(bf16[2,128,5120]{2,1,0:T(8,128)(2,1)} %param.8, f32[2,5120]{1,0:T(2,128)S(1)} %bitcast_convert_fusion.1, bf16[2,128,4096]{2,1,0:T(8,128)(2,1)} %param.7, f32[2,4096]{1,0:T(2,128)S(1)} %bitcast.10), kind=kOutput, calls=%fused_computation | convolution fusion | flops 10765467648 | bytes 46735360 | tf_op jit(solution)/shard_map/dot_general | solution.py:35
  27.4 0.0 copy-start
  27.4 0.0 reduce-scatter.2.cloned.1.call-update
  27.4 194.9 %reduce-scatter.2.cloned.1.call-done = bf16[160,4096]{1,0:T(8,128)(2,1)} async-done(((bf16[5120,4096]{1,0:T(8,128)(2,1)}), bf16[160,4096]{1,0:T(8,128)(2,1)}) %reduce-scatter.2.cloned.1.call-update) | async-done | bytes 1310736 | tf_op jit(solution)/shard_map/reduce_scatter | solution.py:53
  222.3 2.6 fusion.2
  224.9 11.0 %psum.28 = f32[]{:T(128)} all-reduce(f32[]{:T(128)} %fusion.2), channel_id=1, replica_groups=mesh['dp_0'=4,'dp_1'=4,'dp_2'=2,'tensor'=4] {'dp_0'}, use_global_device_ids=true, to_apply=%region_2.0 | all-reduce | flops 1 | bytes 8 | tf_op jit(solution)/shard_map/psum | solution.py:25
  235.9 9.2 %psum.29 = f32[]{:T(128)} all-reduce(f32[]{:T(128)} %psum.28), channel_id=1, replica_groups=mesh['dp_0'=4,'dp_1'=4,'dp_2'=2,'tensor'=4] {'dp_1'}, use_global_device_ids=true, to_apply=%region_3.0 | all-reduce | flops 1 | bytes 8 | tf_op jit(solution)/shard_map/psum | solution.py:25
  245.1 3.1 %psum.30 = f32[]{:T(128)} all-reduce(f32[]{:T(128)} %psum.29), channel_id=1, replica_groups=mesh['dp_0'=4,'dp_1'=4,'dp_2'=2,'tensor'=4] {'dp_2'}, use_global_device_ids=true, to_apply=%region_4.0 | all-reduce | flops 1 | bytes 8 | tf_op jit(solution)/shard_map/psum | solution.py:25
  248.2 11.1 %psum.31 = f32[]{:T(128)} all-reduce(f32[]{:T(128)} %psum.30), channel_id=1, replica_groups=mesh['dp_0'=4,'dp_1'=4,'dp_2'=2,'tensor'=4] {'tensor'}, use_global_device_ids=true, to_apply=%region_5.0 | all-reduce | flops 1 | bytes 8 | tf_op jit(solution)/shard_map/psum | solution.py:25
  260.0 0.0 copy-done
  260.0 7.6 %fusion.6 = (bf16[160,4096]{1,0:T(8,128)(2,1)}, f32[160,4096]{1,0:T(8,128)}, f32[160,4096]{1,0:T(8,128)}, f32[160,4096]{1,0:T(8,128)}) fusion(f32[160,4096]{1,0:T(8,128)S(1)} %copy-done, bf16[160,4096]{1,0:T(8,128)(2,1)} %reduce-scatter.2.cloned.1.call-done, f32[]{:T(128)S(6)} %min.3, f32[160,4096]{1,0:T(8,128)} %param.12, f32[160,4096]{1,0:T(8,128)} %param.11), kind=kLoop, calls=%fused_computation.16 | loop fusion | flops 9175040 | bytes 18350084 | tf_op jit(solution)/shard_map/convert_element_type | solution.py:66
  (1 shorter events, 0.0 us)
Async XLA Ops:
  7.2 215.2 %reduce-scatter.2.cloned.1.call-start = ((), (), s32[]{:S(2)}) async-start(), calls=%async_computation.1 | async-start | bytes 43253760 | tf_op jit(solution)/shard_map/reduce_scatter | solution.py:53
  27.4 232.6 %copy-start = (f32[160,4096]{1,0:T(8,128)S(1)}, f32[160,4096]{1,0:T(8,128)}, u32[]{:S(2)}) copy-start(f32[160,4096]{1,0:T(8,128)} %param.13) | copy-start | bytes 7864324
Sparse Core Ops, SparseCore 0:
  27.5 194.7 reduce-scatter.1
where the time goes:
time: 275 us; the launch traced here: 274 us
  waiting for transfers between devices  195 us (71%)
  blocking collectives  34.4 us (13%)
  matrix products  18.6 us (7%)
  between operations  14.7 us (5%)
  other arithmetic  11.6 us (4%)
    reduce_scatter x1, waiting for transfers between devices, per_device(): lax.psum_scatter(transposed_product(grads_deq, acts_deq).astype(jnp.bfloa...  195 us
    psum x4, blocking collectives, over_axes(): return functools.reduce(lax.psum, axes, shard)  34.4 us
    dot_general x1, matrix products, transposed_product(): lax.dot_general(grads_rows, acts_rows, (((0,), (0,)), ((), ())), preferre...  18.6 us
    convert_element_type x1, other arithmetic, per_device(): weights = new_master.astype(jnp.bfloat16)  7.6 us
  transfers between devices with their start and end apart: 1, of which 1 were waited for; matrix products, arithmetic and copies ran while one was open for 0% of the time, Pallas kernels for 0%

commit v1 on v0

v1 whole, which is shorter than its diff:
```python
import functools

import jax
import jax.numpy as jnp
from jax import lax
from jax.experimental import pallas as pl
from jax.experimental.pallas import tpu as pltpu
from jax.sharding import Mesh
from jax.sharding import PartitionSpec as P

FF = 20480
ROWS = 4096
DP = ("dp_0", "dp_1", "dp_2")
TENSOR_DP = ("tensor", "dp_0", "dp_1", "dp_2")

clip_rms = 1.0
beta_first = 0.9
beta_second = 0.95
learn_rate = 0.003
adam_eps = 1e-08

TOK = 256
HALF = ROWS // 2
TILE = 256
STEPS = HALF // TILE
BLK = 320
OWN = 160
QUART = 128
B_OFF = (2, 1, 3, 0)
BF = jnp.bfloat16
F32 = jnp.float32


def kernel(
    acts_hbm, grads_hbm, ascale, gscale,
    grad_out, factor_out,
    acts_raw, grads_raw, wide, A, S, GO, G, RB, PB, H, RF, PP, acc, NS, N1, N2, N3,
    load_sem, pair_s, pair_r, q_s, q_r, d_s, d_r, y_s, y_r,
    hop_s, hop_r, nbr_s, nbr_r, rel_s, rel_r,
    rh_s, rh_r, rf_s, rf_r, pp_s, pp_r, n_s, n_r,
):
    z = lax.axis_index("dp_0")
    x = lax.axis_index("dp_1")
    c = lax.axis_index("dp_2")
    y = lax.axis_index("tensor")
    a = x + c * (z - x)
    b = z + c * (x - z)

    def gdev(d):
        return (lax.rem(z + c * d, 4), lax.rem(x + (1 - c) * d, 4), c, y)

    def rdev(d, core):
        return (lax.rem(z + (1 - c) * d, 4), lax.rem(x + c * d, 4), core, y)

    def ydev(d):
        return (z, x, c, lax.rem(y + d, 4))

    partner = (z, x, 1 - c, y)
    MESH = pl.DeviceIdType.MESH

    def send(src, dst, ss, rs, dev):
        pltpu.make_async_remote_copy(
            src_ref=src, dst_ref=dst, send_sem=ss, recv_sem=rs, device_id=dev, device_id_type=MESH
        ).start()

    def wait(ref, sem):
        pltpu.make_async_copy(ref, ref, sem).wait()

    def of(i, n):
        return pl.ds(pl.multiple_of(i, n), n)

    load_a = pltpu.make_async_copy(acts_hbm, acts_raw, load_sem.at[0])
    load_g = pltpu.make_async_copy(grads_hbm, grads_raw, load_sem.at[1])
    load_a.start()
    load_g.start()
    barrier = pltpu.get_barrier_semaphore()
    greet = [partner]
    for d in (1, 3):
        for core in (0, 1):
            greet.append((lax.rem(z + d, 4), x, core, y))
            greet.append((z, lax.rem(x + d, 4), core, y))
        greet.append(ydev(d))
    for core in (0, 1):
        greet.append((lax.rem(z + 2, 4), x, core, y))
    greet.append((z, lax.rem(x + 2, 4), c, y))
    greet.append(ydev(2))
    for dev in greet:
        pl.semaphore_signal(barrier, inc=1, device_id=dev, device_id_type=MESH)

    for r in range(ROWS // 128):
        wide[:, r * 128 : (r + 1) * 128] = jnp.broadcast_to(
            ascale[:, r : r + 1].astype(F32), (2, 128)
        )
    load_a.wait()

    def scale_acts(i, which, put):
        cols = pl.ds(pl.multiple_of(which * HALF + i * 512, 512), 512)
        for blk in range(2):
            rows = slice(blk * 128, blk * 128 + 128)
            put(blk, i, (acts_raw[blk, :, cols].astype(F32) * wide[blk : blk + 1, cols]).astype(BF))

    def put_other(blk, i, v):
        S[blk * 128 : blk * 128 + 128, pl.ds(pl.multiple_of(i * 512, 512), 512)] = v

    def put_own(blk, i, v):
        A[0, of(c * TOK + blk * 128, 128), pl.ds(pl.multiple_of(i * 512, 512), 512)] = v

    def other_step(i, _):
        scale_acts(i, 1 - c, put_other)
        return 0

    def own_step(i, _):
        scale_acts(i, c, put_own)
        return 0

    lax.fori_loop(0, HALF // 512, other_step, 0)
    pl.semaphore_wait(barrier, len(greet))
    send(S, A.at[0, of(c * TOK, TOK)], pair_s.at[0], pair_r.at[0], partner)
    lax.fori_loop(0, HALF // 512, own_step, 0)
    wait(A.at[0, of((1 - c) * TOK, TOK)], pair_r.at[0])

    mine = of(y * QUART, QUART)
    lo64 = pl.ds(pl.multiple_of(y * QUART, 64), 64)
    hi64 = pl.ds(pl.multiple_of(y * QUART + 64, 64), 64)
    groups = (pl.ds(TILE, TILE), pl.ds(2 * TILE, HALF - 2 * TILE))

    def q_own(g):
        cols = groups[g]
        send(A.at[0, mine, cols], A.at[3, mine, cols], q_s.at[g, 0], q_r.at[g, 0], gdev(1))
        send(A.at[0, mine, cols], A.at[1, mine, cols], q_s.at[g, 1], q_r.at[g, 1], gdev(3))

    def q_relay(g):
        cols = groups[g]
        wait(A.at[3, mine, cols], q_r.at[g, 0])
        send(A.at[3, lo64, cols], A.at[2, lo64, cols], q_s.at[g, 2], q_r.at[g, 2], gdev(1))
        wait(A.at[1, mine, cols], q_r.at[g, 1])
        send(A.at[1, hi64, cols], A.at[2, hi64, cols], q_s.at[g, 3], q_r.at[g, 3], gdev(3))

    def q_done(g):
        cols = groups[g]
        wait(A.at[2, lo64, cols], q_r.at[g, 2])
        wait(A.at[2, hi64, cols], q_r.at[g, 3])

    def q_drain(g):
        cols = groups[g]
        wait(A.at[0, mine, cols], q_s.at[g, 0])
        wait(A.at[0, mine, cols], q_s.at[g, 1])
        wait(A.at[3, lo64, cols], q_s.at[g, 2])
        wait(A.at[1, hi64, cols], q_s.at[g, 3])

    def tile(t):
        return pl.ds(pl.multiple_of(t * TILE, TILE), TILE)

    three = pl.ds(1, 3)
    below = lax.rem(y + 3, 4)
    above = lax.rem(y + 1, 4)
    y_lo = pl.ds(pl.multiple_of(below * QUART, 64), 64)
    y_hi = pl.ds(pl.multiple_of(above * QUART + 64, 64), 64)
    far = lax.rem(y + 2, 4)
    f_lo = pl.ds(pl.multiple_of(far * QUART, 64), 64)
    f_hi = pl.ds(pl.multiple_of(far * QUART + 64, 64), 64)

    def y_own(u):
        v = A.at[three, mine, tile(u)]
        send(v, v, y_s.at[u, 0], y_r.at[u, 0], ydev(1))
        send(v, v, y_s.at[u, 1], y_r.at[u, 1], ydev(3))

    def y_relay(u):
        wait(A.at[three, of(below * QUART, QUART), tile(u)], y_r.at[u, 0])
        v = A.at[three, y_lo, tile(u)]
        send(v, v, y_s.at[u, 2], y_r.at[u, 2], ydev(1))
        wait(A.at[three, of(above * QUART, QUART), tile(u)], y_r.at[u, 1])
        v = A.at[three, y_hi, tile(u)]
        send(v, v, y_s.at[u, 3], y_r.at[u, 3], ydev(3))

    def y_done(u):
        wait(A.at[three, f_lo, tile(u)], y_r.at[u, 2])
        wait(A.at[three, f_hi, tile(u)], y_r.at[u, 3])

    def y_drain(u):
        wait(A.at[three, mine, tile(u)], y_s.at[u, 0])
        wait(A.at[three, mine, tile(u)], y_s.at[u, 1])
        wait(A.at[three, y_lo, tile(u)], y_s.at[u, 2])
        wait(A.at[three, y_hi, tile(u)], y_s.at[u, 3])

    q_own(0)
    q_own(1)

    load_g.wait()

    def turn(i, _):
        cols = pl.ds(pl.multiple_of(i * 512, 512), 512)
        for blk in range(2):
            v = grads_raw[blk, :, cols].astype(F32) * gscale[blk, :, cols].astype(F32)
            GO[cols, of(c * TOK + blk * 128, 128)] = v.T.astype(BF)
        return 0

    lax.fori_loop(0, 10, turn, 0)
    send(GO.at[:, of(c * TOK, TOK)], GO.at[:, of(c * TOK, TOK)], pair_s.at[1], pair_r.at[1], partner)

    q_relay(0)
    q_relay(1)
    d_cols = pl.ds(0, TILE)
    send(A.at[0, :, d_cols], A.at[3, :, d_cols], d_s.at[0], d_r.at[0], gdev(1))
    send(A.at[0, :, d_cols], A.at[1, :, d_cols], d_s.at[1], d_r.at[1], gdev(3))
    q_done(0)
    y_own(1)

    wait(GO.at[:, of((1 - c) * TOK, TOK)], pair_r.at[1])

    def block(da, p, part, n):
        aa = lax.rem(a + da, 4)
        bb = lax.rem(b + B_OFF[p], 4)
        start = (bb * 4 + aa + c * 3 * (aa - bb)) * BLK + part * OWN
        return pl.ds(pl.multiple_of(start, OWN), n)

    for p in range(4):
        send(GO.at[block(2, p, 0, OWN)], RB.at[0, p], hop_s.at[0, p], hop_r.at[0, p], gdev(1))
        send(GO.at[block(2, p, 1, OWN)], RB.at[1, p], hop_s.at[1, p], hop_r.at[1, p], gdev(3))
    own_copies = [
        pltpu.make_async_copy(GO.at[block(0, p, 0, BLK)], G.at[p, :, pl.ds(0, 512)], load_sem.at[2 + p])
        for p in range(4)
    ]
    for cp in own_copies:
        cp.start()

    q_done(1)
    for u in range(2, STEPS):
        y_own(u)

    d_lo, d_hi = pl.ds(0, 256), pl.ds(256, 256)
    wait(A.at[3, :, d_cols], d_r.at[0])
    send(A.at[3, d_lo, d_cols], A.at[2, d_lo, d_cols], d_s.at[2], d_r.at[2], gdev(1))
    wait(A.at[1, :, d_cols], d_r.at[1])
    send(A.at[1, d_hi, d_cols], A.at[2, d_hi, d_cols], d_s.at[3], d_r.at[3], gdev(3))

    for p in range(4):
        src = GO.at[block(1, p, 0, BLK)]
        send(src, G.at[p, :, pl.ds(1536, 512)], nbr_s.at[0, p], nbr_r.at[0, p], gdev(1))
        src = GO.at[block(3, p, 0, BLK)]
        send(src, G.at[p, :, pl.ds(512, 512)], nbr_s.at[1, p], nbr_r.at[1, p], gdev(3))

    y_relay(1)
    first, second = pl.ds(0, OWN), pl.ds(OWN, OWN)
    slot2 = pl.ds(1024, 512)
    for p in range(4):
        wait(RB.at[0, p], hop_r.at[0, p])
        wait(RB.at[1, p], hop_r.at[1, p])
    send(RB.at[0], G.at[:, first, slot2], rel_s.at[0], rel_r.at[0], gdev(1))
    send(RB.at[1], G.at[:, second, slot2], rel_s.at[1], rel_r.at[1], gdev(3))
    for u in range(2, STEPS):
        y_relay(u)

    for p in range(4):
        own_copies[p].wait()
        wait(G.at[p, :, pl.ds(1536, 512)], nbr_r.at[0, p])
        wait(G.at[p, :, pl.ds(512, 512)], nbr_r.at[1, p])
    wait(G.at[:, first, slot2], rel_r.at[0])
    wait(G.at[:, second, slot2], rel_r.at[1])
    wait(A.at[2, d_lo, d_cols], d_r.at[2])
    wait(A.at[2, d_hi, d_cols], d_r.at[3])
    acc[...] = jnp.zeros_like(acc)

    def out_tile(h, t):
        return pl.ds(pl.multiple_of(h * HALF + t * TILE, TILE), TILE)

    def product(p, t):
        acts = A[:, :, tile(t)].reshape(4 * 512, TILE)
        return jnp.dot(G[p], acts, preferred_element_type=F32).astype(BF)

    def reduce_send(d, part, core, t):
        src = PB.at[1 + d, pl.ds(part * OWN, OWN), tile(t)]
        send(src, RF.at[d, :, out_tile(c, t)], rf_s.at[d, core, t], rf_r.at[d, c, t], rdev(1 + 2 * d, core))

    def add_send(t):
        for d in (0, 1):
            wait(H.at[d, :, tile(t)], rh_r.at[d, t])
            rows = pl.ds(d * OWN, OWN)
            both = PB[1 + d, rows, tile(t)].astype(F32) + H[d, :, tile(t)].astype(F32)
            PB[1 + d, rows, tile(t)] = both.astype(BF)
            reduce_send(d, d, d, t)

    def finish(t):
        wait(PP.at[:, out_tile(1 - c, t)], pp_r.at[t])
        for h in (0, 1):
            cols = out_tile(h, t)
            wait(RF.at[0, :, cols], rf_r.at[0, h, t])
            wait(RF.at[1, :, cols], rf_r.at[1, h, t])
            g = PP[:, cols].astype(F32) + RF[0, :, cols].astype(F32) + RF[1, :, cols].astype(F32)
            grad_out[:, cols] = g
            sq = jnp.sum((g * g).reshape(OWN // 8, 8, TILE), axis=0)
            acc[...] += sq[:, :128] + sq[:, 128:]

    keep = of(c * OWN, OWN)
    give = of((1 - c) * OWN, OWN)

    def step(t, _):
        @pl.when(t >= 1)
        def _():
            y_done(t)

        PB[0, :, tile(t)] = product(0, t)
        send(PB.at[0, first, tile(t)], H.at[0, :, tile(t)], rh_s.at[0, t], rh_r.at[0, t], rdev(1, c))
        send(PB.at[0, second, tile(t)], H.at[1, :, tile(t)], rh_s.at[1, t], rh_r.at[1, t], rdev(3, c))
        PB[1, :, tile(t)] = product(1, t)
        reduce_send(0, 1, 1, t)
        PB[2, :, tile(t)] = product(2, t)
        reduce_send(1, 0, 0, t)
        PB[3, :, tile(t)] = product(3, t)
        send(PB.at[3, give, tile(t)], PP.at[:, out_tile(c, t)], pp_s.at[t], pp_r.at[t], partner)
        PP[:, out_tile(c, t)] = PB[3, keep, tile(t)]

        @pl.when(t >= 1)
        def _():
            add_send(t - 1)

        @pl.when(t >= 3)
        def _():
            finish(t - 3)

        return 0

    lax.fori_loop(0, STEPS, step, 0)
    add_send(STEPS - 1)

    def last(t, _):
        finish(t)
        return 0

    lax.fori_loop(STEPS - 3, STEPS, last, 0)

    NS[0] = acc[...]
    sent = []
    for dz in range(4):
        for dc in range(2):
            i = dz * 2 + dc
            if i:
                dev = (lax.rem(z + dz, 4), x, lax.rem(c + dc, 2), y)
                send(NS.at[0], N1.at[i - 1], n_s.at[i - 1], n_r.at[i - 1], dev)
                sent.append((0, i - 1))
    for i in range(7):
        wait(N1.at[i], n_r.at[i])
    NS[1] = NS[0] + jnp.sum(N1[...], axis=0)
    for i in range(3):
        dev = (z, lax.rem(x + i + 1, 4), c, y)
        send(NS.at[1], N2.at[i], n_s.at[7 + i], n_r.at[7 + i], dev)
        sent.append((1, 7 + i))
    for i in range(3):
        wait(N2.at[i], n_r.at[7 + i])
    NS[2] = NS[1] + jnp.sum(N2[...], axis=0)
    for i in range(3):
        send(NS.at[2], N3.at[i], n_s.at[10 + i], n_r.at[10 + i], ydev(i + 1))
        sent.append((2, 10 + i))

    wait(S, pair_s.at[0])
    wait(GO.at[:, of(c * TOK, TOK)], pair_s.at[1])
    q_drain(0)
    q_drain(1)
    wait(A.at[0, :, d_cols], d_s.at[0])
    wait(A.at[0, :, d_cols], d_s.at[1])
    wait(A.at[3, d_lo, d_cols], d_s.at[2])
    wait(A.at[1, d_hi, d_cols], d_s.at[3])
    for u in range(1, STEPS):
        y_drain(u)
    for p in range(4):
        wait(RB.at[0, p], hop_s.at[0, p])
        wait(RB.at[1, p], hop_s.at[1, p])
        wait(G.at[p, :, pl.ds(1536, 512)], nbr_s.at[0, p])
        wait(G.at[p, :, pl.ds(512, 512)], nbr_s.at[1, p])
    wait(RB.at[0], rel_s.at[0])
    wait(RB.at[1], rel_s.at[1])

    def drain(t, _):
        for d in (0, 1):
            wait(H.at[d, :, tile(t)], rh_s.at[d, t])
            for core in (0, 1):
                wait(H.at[d, :, tile(t)], rf_s.at[d, core, t])
        wait(H.at[0, :, tile(t)], pp_s.at[t])
        return 0

    lax.fori_loop(0, STEPS, drain, 0)
    for i in range(3):
        wait(N3.at[i], n_r.at[10 + i])
    total = jnp.sum(NS[2] + jnp.sum(N3[...], axis=0), keepdims=True)
    limit = clip_rms * jnp.sqrt(jnp.full((1, 1), FF * ROWS, F32))
    factor_out[...] = jnp.broadcast_to(jnp.minimum(1.0, limit / jnp.sqrt(total)), (8, 128))
    for i, k in sent:
        wait(NS.at[i], n_s.at[k])


def owned_gradient(activations, out_grads, act_scale, grad_scale):
    dma = pltpu.SemaphoreType.DMA
    vmem = pltpu.VMEM
    scratch = [
        vmem((2, 128, ROWS), BF),
        vmem((2, 128, 5120), BF),
        vmem((2, ROWS), F32),
        vmem((4, 512, HALF), BF),
        vmem((TOK, HALF), BF),
        vmem((5120, 512), BF),
        vmem((4, BLK, 2048), BF),
        vmem((2, 4, OWN, 512), BF),
        vmem((4, BLK, HALF), BF),
        vmem((2, OWN, HALF), BF),
        vmem((2, OWN, ROWS), BF),
        vmem((OWN, ROWS), BF),
        vmem((8, 128), F32),
        vmem((3, 8, 128), F32),
        vmem((7, 8, 128), F32),
        vmem((3, 8, 128), F32),
        vmem((3, 8, 128), F32),
        dma((6,)),
        dma((2,)), dma((2,)),
        dma((2, 4)), dma((2, 4)),
        dma((4,)), dma((4,)),
        dma((STEPS, 4)), dma((STEPS, 4)),
        dma((2, 4)), dma((2, 4)),
        dma((2, 4)), dma((2, 4)),
        dma((2,)), dma((2,)),
        dma((2, STEPS)), dma((2, STEPS)),
        dma((2, 2, STEPS)), dma((2, 2, STEPS)),
        dma((STEPS,)), dma((STEPS,)),
        dma((13,)), dma((13,)),
    ]
    return pl.pallas_call(
        kernel,
        out_shape=(
            jax.ShapeDtypeStruct((OWN, ROWS), F32),
            jax.ShapeDtypeStruct((8, 128), F32),
        ),
        in_specs=[
            pl.BlockSpec(memory_space=pl.ANY),
            pl.BlockSpec(memory_space=pl.ANY),
            pl.BlockSpec(memory_space=vmem),
            pl.BlockSpec(memory_space=vmem),
        ],
        out_specs=(pl.BlockSpec(memory_space=vmem), pl.BlockSpec(memory_space=vmem)),
        scratch_shapes=scratch,
        compiler_params=pltpu.CompilerParams(
            collective_id=0, has_side_effects=True, vmem_limit_bytes=46 * 1024 * 1024
        ),
        cost_estimate=pl.CostEstimate(
            flops=2 * 8192 * OWN * ROWS, bytes_accessed=8 * 1024 * 1024, transcendentals=0
        ),
        name="owned_gradient",
    )(activations, out_grads, act_scale, grad_scale)


def per_device(activations, out_grads, act_scale, grad_scale, moment, second, master):
    grad_owned, factors = owned_gradient(activations, out_grads, act_scale, grad_scale)
    clipped = factors[0, 0] * grad_owned
    new_moment = beta_first * moment + (1.0 - beta_first) * clipped
    new_second = beta_second * second + (1.0 - beta_second) * clipped * clipped
    new_master = master - learn_rate * new_moment / (jnp.sqrt(new_second) + adam_eps)
    weights = new_master.astype(jnp.bfloat16)
    return (new_moment, new_second, new_master, weights)


def solution(mesh):
    finer = Mesh(
        mesh.devices.reshape(4, 4, 2, mesh.shape["tensor"]), ("dp_0", "dp_1", "dp_2", "tensor")
    )
    in_specs = (
        P(DP, None, None),
        P(DP, None, "tensor"),
        P(DP, None),
        P(DP, None, "tensor"),
        P(TENSOR_DP, None),
        P(TENSOR_DP, None),
        P(TENSOR_DP, None),
    )
    out_specs = (P(TENSOR_DP, None), P(TENSOR_DP, None), P(TENSOR_DP, None), P(TENSOR_DP, None))
    return jax.shard_map(
        per_device, mesh=finer, in_specs=in_specs, out_specs=out_specs, check_vma=False
    )
```

time: 275 us -> 111 us (0.40)
  waiting for transfers between devices: 195 us -> 0 us
  Pallas kernels: 0 us -> 99.8 us
  blocking collectives: 34.4 us -> 0 us
  matrix products: 18.6 us -> 0 us
  between operations: 14.7 us -> 0.66 us
  other arithmetic: 11.6 us -> 5.22 us
  local copies, waits for them, and re-layouts: 0.1 us -> 5.26 us
    reduce_scatter x1 -> x0, waiting for transfers between devices: 195 us -> none  [per_device(): lax.psum_scatter(transposed_product(grads_deq, acts_deq).astype(jnp.bfloa...]
    pallas_call x0 -> x1, Pallas kernels: none -> 99.8 us  [owned_gradient(): pl.pallas_call(kernel, out_shape=(jax.ShapeDtypeStruct((OWN, ROWS), F32),...]
    psum x4 -> x0, blocking collectives: 34.4 us -> none  [over_axes(): return functools.reduce(lax.psum, axes, shard)]
    dot_general x1 -> x0, matrix products: 18.6 us -> none  [transposed_product(): lax.dot_general(grads_rows, acts_rows, (((0,), (0,)), ((), ())), preferre...]
    unnamed x4 -> x13, local copies, waits for them, and re-layouts: 0.1 us -> 4.75 us
  transfers between devices with their start and end apart: 1 -> 0, of which waited for: 1 -> 0; matrix products, arithmetic and copies ran while one was open for 0% -> 0% of each run, Pallas kernels for 0% -> 0%
where the time goes in v1:
time: 111 us
  Pallas kernels  99.8 us (90%)
  local copies, waits for them, and re-layouts  5.26 us (5%)
  other arithmetic  5.22 us (5%)
    pallas_call x1, Pallas kernels, owned_gradient(): pl.pallas_call(kernel, out_shape=(jax.ShapeDtypeStruct((OWN, ROWS), F32),...  99.8 us
    convert_element_type x1, other arithmetic, per_device(): weights = new_master.astype(jnp.bfloat16)  5.22 us
    unnamed x13, local copies, waits for them, and re-layouts  4.75 us

profile of v1, /device:TPU:0, one launch (start us, length us, event | category | flops | bytes accessed | tf_op | source)
XLA Modules:
  0.0 110.9 jit_solution(1478455458217299198)
XLA Ops:
  0.6 0.8 copy.11.gscale
  1.4 0.0 copy-start
  1.4 1.7 %copy-done = bf16[2,128,5120]{2,1,0:T(8,128)(2,1)S(1)} copy-done((bf16[2,128,5120]{2,1,0:T(8,128)(2,1)S(1)}, bf16[2,128,5120]{2,1,0:T(8,128)(2,1)}, u32[]{:S(2)}) %copy-start) | copy-done | bytes 2621464
  3.1 0.0 copy-start.1
  3.1 1.6 %copy-done.1 = bf16[2,128,4096]{2,1,0:T(8,128)(2,1)S(1)} copy-done((bf16[2,128,4096]{2,1,0:T(8,128)(2,1)S(1)}, bf16[2,128,4096]{2,1,0:T(8,128)(2,1)}, u32[]{:S(2)}) %copy-start.1) | copy-done | bytes 2097176
  4.7 0.0 copy-start.2
  4.7 0.7 copy-done.2
  5.4 0.0 copy-start.3
  5.4 0.0 copy-start.4
  5.4 0.0 copy-start.5
  5.4 99.8 %owned_gradient.1 = (f32[160,4096]{1,0:T(8,128)S(1)}, f32[8,128]{1,0:T(8,128)S(1)}) custom-call(bf16[2,128,4096]{2,1,0:T(8,128)(2,1)S(1)} %copy-done.1, bf16[2,128,5120]{2,1,0:T(8,128)(2,1)S(1)} %copy-done, bf16[2,32]{1,0:T(2,128)(2,1)S(1)} %copy-done.2, bf16[2,1,5120]{2,1,0:T(2,128)(2,1)S(1)} %copy.11.gscale), custom_call_target="tpu_custom_call" | custom-call | flops 10737418240 | bytes 8388608 | tf_op jit(solution)/shard_map/owned_gradient/pallas_call | solution.py:425
  105.2 0.5 slice.3
  105.7 0.0 copy-done.3
  105.7 0.0 copy-done.4
  105.7 0.0 copy-done.5
  105.7 5.2 %fusion.1 = (bf16[160,4096]{1,0:T(8,128)(2,1)}, f32[160,4096]{1,0:T(8,128)}, f32[160,4096]{1,0:T(8,128)}, f32[160,4096]{1,0:T(8,128)}) fusion(f32[160,4096]{1,0:T(8,128)S(1)} %copy-done.3, f32[160,4096]{1,0:T(8,128)S(1)} %get-tuple-element.7, f32[]{:T(128)} %bitcast, f32[160,4096]{1,0:T(8,128)S(1)} %copy-done.4, f32[160,4096]{1,0:T(8,128)S(1)} %copy-done.5), kind=kLoop, calls=%fused_computation.4 | loop fusion | flops 8519680 | bytes 19660804 | tf_op jit(solution)/shard_map/convert_element_type | solution.py:455
Async XLA Ops:
  1.4 1.7 %copy-start = (bf16[2,128,5120]{2,1,0:T(8,128)(2,1)S(1)}, bf16[2,128,5120]{2,1,0:T(8,128)(2,1)}, u32[]{:S(2)}) copy-start(bf16[2,128,5120]{2,1,0:T(8,128)(2,1)} %grads_hbm.1) | copy-start | bytes 7864324
  3.1 1.6 %copy-start.1 = (bf16[2,128,4096]{2,1,0:T(8,128)(2,1)S(1)}, bf16[2,128,4096]{2,1,0:T(8,128)(2,1)}, u32[]{:S(2)}) copy-start(bf16[2,128,4096]{2,1,0:T(8,128)(2,1)} %acts_hbm.1) | copy-start | bytes 6291460
  4.7 0.7 copy-start.2
  5.4 100.3 %copy-start.3 = (f32[160,4096]{1,0:T(8,128)S(1)}, f32[160,4096]{1,0:T(8,128)}, u32[]{:S(2)}) copy-start(f32[160,4096]{1,0:T(8,128)} %param.13) | copy-start | bytes 7864324
  5.4 100.3 %copy-start.4 = (f32[160,4096]{1,0:T(8,128)S(1)}, f32[160,4096]{1,0:T(8,128)}, u32[]{:S(2)}) copy-start(f32[160,4096]{1,0:T(8,128)} %param.12) | copy-start | bytes 7864324
  5.4 100.3 %copy-start.5 = (f32[160,4096]{1,0:T(8,128)S(1)}, f32[160,4096]{1,0:T(8,128)}, u32[]{:S(2)}) copy-start(f32[160,4096]{1,0:T(8,128)} %param.11) | copy-start | bytes 7864324

commit v2 on v1

v2 whole, which is shorter than its diff:
```python
import functools

import jax
import jax.numpy as jnp
from jax import lax
from jax.experimental import pallas as pl
from jax.experimental.pallas import tpu as pltpu
from jax.sharding import Mesh
from jax.sharding import PartitionSpec as P

FF = 20480
ROWS = 4096
DP = ("dp_0", "dp_1", "dp_2")
TENSOR_DP = ("tensor", "dp_0", "dp_1", "dp_2")

clip_rms = 1.0
beta_first = 0.9
beta_second = 0.95
learn_rate = 0.003
adam_eps = 1e-08

TOK = 256
HALF = ROWS // 2
TILE = 256
STEPS = HALF // TILE
BLK = 320
OWN = 160
QUART = 128
B_OFF = (2, 1, 3, 0)
BF = jnp.bfloat16
F32 = jnp.float32


def kernel(
    acts_hbm, grads_hbm, ascale_hbm, gscale_hbm,
    grad_out, factor_out,
    acts_raw, grads_raw, ascale, gscale, wide, A, S, GO, G, RB, PB, H, RF, PP, GR, acc, NS, N1, N2, N3,
    load_sem, own_sem, pair_s, pair_r, q_s, q_r, y_s, y_r,
    hop_s, hop_r, nbr_s, nbr_r, rel_s, rel_r,
    rh_s, rh_r, rf_s, rf_r, pp_s, pp_r, out_sem, n_s, n_r,
):
    z = lax.axis_index("dp_0")
    x = lax.axis_index("dp_1")
    c = lax.axis_index("dp_2")
    y = lax.axis_index("tensor")
    a = x + c * (z - x)
    b = z + c * (x - z)

    def gdev(d):
        return (lax.rem(z + c * d, 4), lax.rem(x + (1 - c) * d, 4), c, y)

    def rdev(d, core):
        return (lax.rem(z + (1 - c) * d, 4), lax.rem(x + c * d, 4), core, y)

    def ydev(d):
        return (z, x, c, lax.rem(y + d, 4))

    partner = (z, x, 1 - c, y)
    MESH = pl.DeviceIdType.MESH

    def send(src, dst, ss, rs, dev):
        pltpu.make_async_remote_copy(
            src_ref=src, dst_ref=dst, send_sem=ss, recv_sem=rs, device_id=dev, device_id_type=MESH
        ).start()

    def wait(ref, sem):
        pltpu.make_async_copy(ref, ref, sem).wait()

    def of(i, n):
        return pl.ds(pl.multiple_of(i, n), n)

    barrier = pltpu.get_barrier_semaphore()
    greet = [partner]
    for d in (1, 3):
        for core in (0, 1):
            greet.append((lax.rem(z + d, 4), x, core, y))
            greet.append((z, lax.rem(x + d, 4), core, y))
        greet.append(ydev(d))
    for dev in greet:
        pl.semaphore_signal(barrier, inc=1, device_id=dev, device_id_type=MESH)
    loads = [
        pltpu.make_async_copy(src, dst, load_sem.at[i])
        for i, (src, dst) in enumerate(
            ((ascale_hbm, ascale), (acts_hbm, acts_raw), (gscale_hbm, gscale), (grads_hbm, grads_raw))
        )
    ]
    for load in loads:
        load.start()

    loads[0].wait()
    for r in range(ROWS // 128):
        wide[:, r * 128 : (r + 1) * 128] = jnp.broadcast_to(
            ascale[:, r : r + 1].astype(F32), (2, 128)
        )
    loads[1].wait()

    def scale_step(i, _):
        dst = pl.ds(pl.multiple_of(i * 512, 512), 512)
        for which, put in ((1 - c, 0), (c, 1)):
            cols = pl.ds(pl.multiple_of(which * HALF + i * 512, 512), 512)
            for blk in range(2):
                v = (acts_raw[blk, :, cols].astype(F32) * wide[blk : blk + 1, cols]).astype(BF)
                v = v.reshape(2, 64, 512)
                rows = pl.ds(2 * blk, 2)
                if put:
                    A[0, c, rows, :, dst] = v
                else:
                    S[rows, :, dst] = v
        return 0

    lax.fori_loop(0, HALF // 512, scale_step, 0)

    def turn(i, _):
        cols = pl.ds(pl.multiple_of(i * 512, 512), 512)
        for blk in range(2):
            v = grads_raw[blk, :, cols].astype(F32) * gscale[blk : blk + 1, cols].astype(F32)
            GO[cols, of(c * TOK + blk * 128, 128)] = v.T.astype(BF)
        return 0

    pl.semaphore_wait(barrier, len(greet))

    groups = (pl.ds(0, TILE), pl.ds(TILE, 2 * TILE), pl.ds(3 * TILE, HALF - 3 * TILE))
    pieces = (pl.ds(0, TILE), pl.ds(TILE, HALF - TILE))
    for i in range(2):
        send(S.at[:, :, pieces[i]], A.at[0, c, :, :, pieces[i]], pair_s.at[i], pair_r.at[i], partner)

    def q_own(g, k):
        who = c + k * (1 - 2 * c)
        src = A.at[0, who, y, :, groups[g]]
        send(src, A.at[2, who, y, :, groups[g]], q_s.at[g, 0, k], q_r.at[g, 0, who], gdev(1))
        send(src, A.at[1, who, y, :, groups[g]], q_s.at[g, 1, k], q_r.at[g, 1, who], gdev(3))

    def q_relay(g):
        cols = groups[g]
        wait(A.at[2, 0, y, :, cols], q_r.at[g, 0, 0])
        send(A.at[2, 0, y, :, cols], A.at[3, 0, y, :, cols], q_s.at[g, 2, 0], q_r.at[g, 2, 0], gdev(1))
        wait(A.at[1, 1, y, :, cols], q_r.at[g, 1, 1])
        send(A.at[1, 1, y, :, cols], A.at[3, 1, y, :, cols], q_s.at[g, 2, 1], q_r.at[g, 2, 1], gdev(3))

    def q_near(g):
        cols = groups[g]
        wait(A.at[2, 1, y, :, cols], q_r.at[g, 0, 1])
        wait(A.at[1, 0, y, :, cols], q_r.at[g, 1, 0])

    def q_far(g):
        cols = groups[g]
        wait(A.at[3, 0, y, :, cols], q_r.at[g, 2, 0])
        wait(A.at[3, 1, y, :, cols], q_r.at[g, 2, 1])

    def q_drain(g):
        v = A.at[0, 0, y, :, groups[g]]
        for i in range(3):
            for k in range(2):
                wait(v, q_s.at[g, i, k])

    def tile(t):
        return pl.ds(pl.multiple_of(t * TILE, TILE), TILE)

    parts = (pl.ds(1, 2), pl.ds(3, 1))
    both = pl.ds(0, 2)
    below = lax.rem(y + 3, 4)
    above = lax.rem(y + 1, 4)
    far = lax.rem(y + 2, 4)

    def y_own(u, i):
        v = A.at[parts[i], both, y, :, tile(u)]
        send(v, v, y_s.at[u, i, 0], y_r.at[u, i, 0], ydev(1))
        send(v, v, y_s.at[u, i, 1], y_r.at[u, i, 1], ydev(3))

    def y_relay(u):
        for i in range(2):
            wait(A.at[parts[i], both, below, :, tile(u)], y_r.at[u, i, 0])
            v = A.at[parts[i], 0, below, :, tile(u)]
            send(v, v, y_s.at[u, i, 2], y_r.at[u, i, 2], ydev(1))
            wait(A.at[parts[i], both, above, :, tile(u)], y_r.at[u, i, 1])
            v = A.at[parts[i], 1, above, :, tile(u)]
            send(v, v, y_s.at[u, i, 3], y_r.at[u, i, 3], ydev(3))

    def y_done(u):
        for i in range(2):
            wait(A.at[parts[i], 0, far, :, tile(u)], y_r.at[u, i, 2])
            wait(A.at[parts[i], 1, far, :, tile(u)], y_r.at[u, i, 3])

    def y_drain(u):
        for i in range(2):
            wait(A.at[parts[i], both, y, :, tile(u)], y_s.at[u, i, 0])
            wait(A.at[parts[i], both, y, :, tile(u)], y_s.at[u, i, 1])
            wait(A.at[parts[i], 0, below, :, tile(u)], y_s.at[u, i, 2])
            wait(A.at[parts[i], 1, above, :, tile(u)], y_s.at[u, i, 3])

    q_own(0, 0)
    q_own(1, 0)
    wait(A.at[0, 1 - c, :, :, pieces[0]], pair_r.at[0])
    q_own(0, 1)
    q_own(2, 0)

    loads[2].wait()
    loads[3].wait()
    lax.fori_loop(0, 10, turn, 0)
    half = GO.at[:, of(c * TOK, TOK)]
    send(half, half, pair_s.at[2], pair_r.at[2], partner)
    wait(A.at[0, 1 - c, :, :, pieces[1]], pair_r.at[1])
    q_own(1, 1)
    q_relay(0)
    q_own(2, 1)
    q_near(0)
    y_own(0, 0)

    def block(da, p, part, n):
        aa = lax.rem(a + da, 4)
        bb = lax.rem(b + B_OFF[p], 4)
        start = (bb * 4 + aa + c * 3 * (aa - bb)) * BLK + part * OWN
        return pl.ds(pl.multiple_of(start, OWN), n)

    wait(GO.at[:, of((1 - c) * TOK, TOK)], pair_r.at[2])
    own_copies = [
        pltpu.make_async_copy(GO.at[block(0, p, 0, BLK)], G.at[p, :, pl.ds(0, 512)], own_sem.at[p])
        for p in range(4)
    ]

    def hop(p):
        send(GO.at[block(2, p, 0, OWN)], RB.at[0, p], hop_s.at[0, p], hop_r.at[0, p], gdev(1))
        send(GO.at[block(2, p, 1, OWN)], RB.at[1, p], hop_s.at[1, p], hop_r.at[1, p], gdev(3))

    slot1, slot2, slot3 = pl.ds(512, 512), pl.ds(1024, 512), pl.ds(1536, 512)
    first, second = pl.ds(0, OWN), pl.ds(OWN, OWN)

    def near(p):
        send(GO.at[block(1, p, 0, BLK)], G.at[p, :, slot2], nbr_s.at[0, p], nbr_r.at[0, p], gdev(1))
        send(GO.at[block(3, p, 0, BLK)], G.at[p, :, slot1], nbr_s.at[1, p], nbr_r.at[1, p], gdev(3))

    def hop_relay(p):
        wait(RB.at[0, p], hop_r.at[0, p])
        send(RB.at[0, p], G.at[p, first, slot3], rel_s.at[0, p], rel_r.at[0, p], gdev(1))
        wait(RB.at[1, p], hop_r.at[1, p])
        send(RB.at[1, p], G.at[p, second, slot3], rel_s.at[1, p], rel_r.at[1, p], gdev(3))

    def block_done(p):
        own_copies[p].wait()
        wait(G.at[p, :, slot2], nbr_r.at[0, p])
        wait(G.at[p, :, slot1], nbr_r.at[1, p])
        wait(G.at[p, first, slot3], rel_r.at[0, p])
        wait(G.at[p, second, slot3], rel_r.at[1, p])

    q_relay(1)
    hop(0)
    for cp in own_copies:
        cp.start()
    q_far(0)
    y_own(0, 1)
    q_near(1)
    y_own(1, 0)
    q_relay(2)
    for p in range(1, 4):
        hop(p)
    near(0)
    q_far(1)
    y_own(1, 1)
    y_relay(0)
    y_own(2, 0)
    y_own(2, 1)
    hop_relay(0)
    near(1)
    hop_relay(1)
    near(2)
    q_near(2)
    q_far(2)
    y_relay(1)
    y_own(3, 0)
    y_own(3, 1)
    hop_relay(2)
    near(3)
    hop_relay(3)
    for u in range(2, 4):
        y_relay(u)
        y_own(u + 2, 0)
        y_own(u + 2, 1)

    for p in range(3):
        block_done(p)
    acc[...] = jnp.zeros_like(acc)

    def out_tile(h, t):
        return pl.ds(pl.multiple_of(h * HALF + t * TILE, TILE), TILE)

    def product(p, n, t):
        acts = A[:, :, :, :, tile(t)].reshape(4 * 512, TILE)
        left = G[p : p + n].reshape(n * BLK, 2048)
        return jnp.dot(left, acts, preferred_element_type=F32).astype(BF).reshape(n, BLK, TILE)

    def reduce_send(d, part, core, t):
        src = PB.at[1 + d, pl.ds(part * OWN, OWN), tile(t)]
        send(src, RF.at[d, :, out_tile(c, t)], rf_s.at[d, core, t], rf_r.at[d, c, t], rdev(1 + 2 * d, core))

    def add_send(t):
        for d in (0, 1):
            wait(H.at[d, :, tile(t)], rh_r.at[d, t])
            rows = pl.ds(d * OWN, OWN)
            total = PB[1 + d, rows, tile(t)].astype(F32) + H[d, :, tile(t)].astype(F32)
            PB[1 + d, rows, tile(t)] = total.astype(BF)
            reduce_send(d, d, d, t)

    keep = of(c * OWN, OWN)
    give = of((1 - c) * OWN, OWN)

    def own_block(t):
        PB[3, :, tile(t)] = product(3, 1, t)[0]
        send(PB.at[3, give, tile(t)], PP.at[:, out_tile(c, t)], pp_s.at[t], pp_r.at[t], partner)
        PP[:, out_tile(c, t)] = PB[3, keep, tile(t)]

    def copy_out(h, t):
        cols = out_tile(h, t)
        return pltpu.make_async_copy(GR.at[:, cols], grad_out.at[:, cols], out_sem.at[h, t])

    def finish(t):
        wait(PP.at[:, out_tile(1 - c, t)], pp_r.at[t])
        for h in (0, 1):
            cols = out_tile(h, t)
            wait(RF.at[0, :, cols], rf_r.at[0, h, t])
            wait(RF.at[1, :, cols], rf_r.at[1, h, t])
            g = PP[:, cols].astype(F32) + RF[0, :, cols].astype(F32) + RF[1, :, cols].astype(F32)
            GR[:, cols] = g
            copy_out(h, t).start()
            sq = jnp.sum((g * g).reshape(OWN // 8, 8, TILE), axis=0)
            acc[...] += sq[:, :128] + sq[:, 128:]

    def step(t, _):
        y_done(t)
        PB[0:3, :, tile(t)] = product(0, 3, t)
        send(PB.at[0, first, tile(t)], H.at[0, :, tile(t)], rh_s.at[0, t], rh_r.at[0, t], rdev(1, c))
        send(PB.at[0, second, tile(t)], H.at[1, :, tile(t)], rh_s.at[1, t], rh_r.at[1, t], rdev(3, c))
        reduce_send(0, 1, 1, t)
        reduce_send(1, 0, 0, t)

        @pl.when(lax.rem(t, 2) == 0)
        def _():
            u = 4 + lax.div(t, 2)
            y_relay(u)

            @pl.when(u < STEPS - 2)
            def _():
                y_own(u + 2, 0)
                y_own(u + 2, 1)

        @pl.when(t >= 1)
        def _():
            add_send(t - 1)

        @pl.when(t == 2)
        def _():
            block_done(3)

        @pl.when(t >= 2)
        def _():
            own_block(t - 2)

        @pl.when(t >= 3)
        def _():
            finish(t - 3)

        return 0

    lax.fori_loop(0, STEPS, step, 0)
    own_block(STEPS - 2)
    own_block(STEPS - 1)
    add_send(STEPS - 1)

    def last(t, _):
        finish(t)
        return 0

    lax.fori_loop(STEPS - 3, STEPS, last, 0)

    NS[0] = acc[...]
    sent = []
    for dz in range(4):
        for dc in range(2):
            i = dz * 2 + dc
            if i:
                dev = (lax.rem(z + dz, 4), x, lax.rem(c + dc, 2), y)
                send(NS.at[0], N1.at[i - 1], n_s.at[i - 1], n_r.at[i - 1], dev)
                sent.append((0, i - 1))
    for i in range(7):
        wait(N1.at[i], n_r.at[i])
    NS[1] = NS[0] + jnp.sum(N1[...], axis=0)
    for i in range(3):
        dev = (z, lax.rem(x + i + 1, 4), c, y)
        send(NS.at[1], N2.at[i], n_s.at[7 + i], n_r.at[7 + i], dev)
        sent.append((1, 7 + i))
    for i in range(3):
        wait(N2.at[i], n_r.at[7 + i])
    NS[2] = NS[1] + jnp.sum(N2[...], axis=0)
    for i in range(3):
        send(NS.at[2], N3.at[i], n_s.at[10 + i], n_r.at[10 + i], ydev(i + 1))
        sent.append((2, 10 + i))

    for i in range(2):
        wait(S.at[:, :, pieces[i]], pair_s.at[i])
    wait(half, pair_s.at[2])
    for g in range(3):
        q_drain(g)
    for p in range(4):
        for d in (0, 1):
            wait(RB.at[d, p], hop_s.at[d, p])
            wait(RB.at[d, p], rel_s.at[d, p])
            wait(G.at[p, :, slot1], nbr_s.at[d, p])

    def drain(t, _):
        y_drain(t)
        for d in (0, 1):
            wait(H.at[d, :, tile(t)], rh_s.at[d, t])
            for core in (0, 1):
                wait(H.at[d, :, tile(t)], rf_s.at[d, core, t])
            copy_out(d, t).wait()
        wait(H.at[0, :, tile(t)], pp_s.at[t])
        return 0

    lax.fori_loop(0, STEPS, drain, 0)
    for i in range(3):
        wait(N3.at[i], n_r.at[10 + i])
    total = jnp.sum(NS[2] + jnp.sum(N3[...], axis=0), keepdims=True)
    limit = clip_rms * jnp.sqrt(jnp.full((1, 1), FF * ROWS, F32))
    factor_out[...] = jnp.minimum(1.0, limit / jnp.sqrt(total))
    for i, k in sent:
        wait(NS.at[i], n_s.at[k])


def owned_gradient(activations, out_grads, act_scale, grad_scale):
    dma = pltpu.SemaphoreType.DMA
    vmem = pltpu.VMEM
    scratch = [
        vmem((2, 128, ROWS), BF),
        vmem((2, 128, 5120), BF),
        vmem((2, ROWS // 128), BF),
        vmem((2, 5120), BF),
        vmem((2, ROWS), F32),
        vmem((4, 2, 4, 64, HALF), BF),
        vmem((4, 64, HALF), BF),
        vmem((5120, 512), BF),
        vmem((4, BLK, 2048), BF),
        vmem((2, 4, OWN, 512), BF),
        vmem((4, BLK, HALF), BF),
        vmem((2, OWN, HALF), BF),
        vmem((2, OWN, ROWS), BF),
        vmem((OWN, ROWS), BF),
        vmem((OWN, ROWS), F32),
        vmem((8, 128), F32),
        vmem((3, 8, 128), F32),
        vmem((7, 8, 128), F32),
        vmem((3, 8, 128), F32),
        vmem((3, 8, 128), F32),
        dma((4,)),
        dma((4,)),
        dma((3,)), dma((3,)),
        dma((3, 3, 2)), dma((3, 3, 2)),
        dma((STEPS, 2, 4)), dma((STEPS, 2, 4)),
        dma((2, 4)), dma((2, 4)),
        dma((2, 4)), dma((2, 4)),
        dma((2, 4)), dma((2, 4)),
        dma((2, STEPS)), dma((2, STEPS)),
        dma((2, 2, STEPS)), dma((2, 2, STEPS)),
        dma((STEPS,)), dma((STEPS,)),
        dma((2, STEPS)),
        dma((13,)), dma((13,)),
    ]
    return pl.pallas_call(
        kernel,
        out_shape=(
            jax.ShapeDtypeStruct((OWN, ROWS), F32),
            jax.ShapeDtypeStruct((1, 1), F32),
        ),
        in_specs=[pl.BlockSpec(memory_space=pltpu.HBM)] * 4,
        out_specs=(pl.BlockSpec(memory_space=pl.ANY), pl.BlockSpec(memory_space=vmem)),
        scratch_shapes=scratch,
        compiler_params=pltpu.CompilerParams(
            collective_id=0, has_side_effects=True, vmem_limit_bytes=46 * 1024 * 1024
        ),
        cost_estimate=pl.CostEstimate(
            flops=2 * 8192 * OWN * ROWS, bytes_accessed=8 * 1024 * 1024, transcendentals=0
        ),
        name="owned_gradient",
    )(*(
        pltpu.with_memory_space_constraint(v, pltpu.HBM)
        for v in (activations, out_grads, act_scale, grad_scale.reshape(2, 5120))
    ))


def per_device(activations, out_grads, act_scale, grad_scale, moment, second, master):
    grad_owned, factors = owned_gradient(activations, out_grads, act_scale, grad_scale)
    clipped = factors.reshape(()) * grad_owned
    new_moment = beta_first * moment + (1.0 - beta_first) * clipped
    new_second = beta_second * second + (1.0 - beta_second) * clipped * clipped
    new_master = master - learn_rate * new_moment / (jnp.sqrt(new_second) + adam_eps)
    weights = new_master.astype(jnp.bfloat16)
    return (new_moment, new_second, new_master, weights)


def solution(mesh):
    finer = Mesh(
        mesh.devices.reshape(4, 4, 2, mesh.shape["tensor"]), ("dp_0", "dp_1", "dp_2", "tensor")
    )
    in_specs = (
        P(DP, None, None),
        P(DP, None, "tensor"),
        P(DP, None),
        P(DP, None, "tensor"),
        P(TENSOR_DP, None),
        P(TENSOR_DP, None),
        P(TENSOR_DP, None),
    )
    out_specs = (P(TENSOR_DP, None), P(TENSOR_DP, None), P(TENSOR_DP, None), P(TENSOR_DP, None))
    return jax.shard_map(
        per_device, mesh=finer, in_specs=in_specs, out_specs=out_specs, check_vma=False
    )
```

time: 111 us -> 97.1 us (0.87)
  Pallas kernels: 99.8 us -> 91 us
  local copies, waits for them, and re-layouts: 5.26 us -> 0.01 us
    pallas_call x1, Pallas kernels: 99.8 us -> 91 us  [owned_gradient(): pl.pallas_call(kernel, out_shape=(jax.ShapeDtypeStruct((OWN, ROWS), F32),...]
    unnamed x13 -> x6, local copies, waits for them, and re-layouts: 4.75 us -> 0.01 us
where the time goes in v2:
time: 97.1 us; the launch traced here: 97 us
  Pallas kernels  91 us (94%)
  other arithmetic  5.34 us (5%)
    pallas_call x1, Pallas kernels, owned_gradient(): pl.pallas_call(kernel, out_shape=(jax.ShapeDtypeStruct((OWN, ROWS), F32),...  91 us
    convert_element_type x1, other arithmetic, per_device(): weights = new_master.astype(jnp.bfloat16)  5.34 us

profile of v2, /device:TPU:0, one launch (start us, length us, event | category | flops | bytes accessed | tf_op | source)
XLA Modules:
  0.0 97.0 jit_solution(5454044169376017738)
XLA Ops:
  0.6 0.0 copy-start
  0.6 0.0 copy-start.1
  0.7 0.0 copy-start.2
  0.7 91.0 %owned_gradient.1 = (f32[160,4096]{1,0:T(8,128)S(1)}, f32[1,1]{1,0:T(1,128)}) custom-call(bf16[2,128,4096]{2,1,0:T(8,128)(2,1)} %acts_hbm.1, bf16[2,128,5120]{2,1,0:T(8,128)(2,1)} %grads_hbm.1, bf16[2,32]{1,0:T(2,128)(2,1)} %ascale_hbm.1, bf16[2,5120]{1,0:T(2,128)(2,1)} %bitcast.2), custom_call_target="tpu_custom_call" | custom-call | flops 10737418240 | bytes 8388608 | tf_op jit(solution)/shard_map/owned_gradient/pallas_call | solution.py:466
  91.6 0.0 copy-done
  91.7 0.0 copy-done.1
  91.7 0.0 copy-done.2
  91.7 5.3 %fusion.1 = (bf16[160,4096]{1,0:T(8,128)(2,1)}, f32[160,4096]{1,0:T(8,128)}, f32[160,4096]{1,0:T(8,128)}, f32[160,4096]{1,0:T(8,128)}) fusion(f32[160,4096]{1,0:T(8,128)S(1)} %copy-done, f32[160,4096]{1,0:T(8,128)S(1)} %get-tuple-element.7, f32[]{:T(128)} %bitcast.1, f32[160,4096]{1,0:T(8,128)S(1)} %copy-done.1, f32[160,4096]{1,0:T(8,128)S(1)} %copy-done.2), kind=kLoop, calls=%fused_computation.4 | loop fusion | flops 8519680 | bytes 19660804 | tf_op jit(solution)/shard_map/convert_element_type | solution.py:494
Async XLA Ops:
  0.6 91.0 %copy-start = (f32[160,4096]{1,0:T(8,128)S(1)}, f32[160,4096]{1,0:T(8,128)}, u32[]{:S(2)}) copy-start(f32[160,4096]{1,0:T(8,128)} %param.13) | copy-start | bytes 7864324
  0.6 91.0 %copy-start.1 = (f32[160,4096]{1,0:T(8,128)S(1)}, f32[160,4096]{1,0:T(8,128)}, u32[]{:S(2)}) copy-start(f32[160,4096]{1,0:T(8,128)} %param.12) | copy-start | bytes 7864324
  0.7 91.0 %copy-start.2 = (f32[160,4096]{1,0:T(8,128)S(1)}, f32[160,4096]{1,0:T(8,128)}, u32[]{:S(2)}) copy-start(f32[160,4096]{1,0:T(8,128)} %param.11) | copy-start | bytes 7864324

commit v3 on v2

v3 whole, which is shorter than its diff:
```python
import functools

import jax
import jax.numpy as jnp
from jax import lax
from jax.experimental import pallas as pl
from jax.experimental.pallas import tpu as pltpu
from jax.sharding import Mesh
from jax.sharding import PartitionSpec as P

FF = 20480
ROWS = 4096
DP = ("dp_0", "dp_1", "dp_2")
TENSOR_DP = ("tensor", "dp_0", "dp_1", "dp_2")

clip_rms = 1.0
beta_first = 0.9
beta_second = 0.95
learn_rate = 0.003
adam_eps = 1e-08

TOK = 256
HALF = ROWS // 2
TILE = 256
STEPS = HALF // TILE
BLK = 320
OWN = 160
QUART = 128
B_OFF = (2, 1, 3, 0)
BF = jnp.bfloat16
F32 = jnp.float32


def kernel(
    acts_hbm, grads_hbm, ascale_hbm, gscale_hbm,
    grad_out, factor_out,
    acts_raw, grads_raw, ascale, gscale, wide, A, S, GO, G, RB, PB, H, RF, PP, GR, acc, NS, N1,
    load_sem, own_sem, pair_s, pair_r, q_s, q_r, y_s, y_r,
    hop_s, hop_r, nbr_s, rel_s, blk_r,
    rh_s, rh_r, rf_s, pp_s, fin_r, out_sem, n_s, n_r,
):
    z = lax.axis_index("dp_0")
    x = lax.axis_index("dp_1")
    c = lax.axis_index("dp_2")
    y = lax.axis_index("tensor")
    a = x + c * (z - x)
    b = z + c * (x - z)

    def gdev(d):
        return (lax.rem(z + c * d, 4), lax.rem(x + (1 - c) * d, 4), c, y)

    def rdev(d, core):
        return (lax.rem(z + (1 - c) * d, 4), lax.rem(x + c * d, 4), core, y)

    def ydev(d):
        return (z, x, c, lax.rem(y + d, 4))

    partner = (z, x, 1 - c, y)
    MESH = pl.DeviceIdType.MESH

    def send(src, dst, ss, rs, dev):
        pltpu.make_async_remote_copy(
            src_ref=src, dst_ref=dst, send_sem=ss, recv_sem=rs, device_id=dev, device_id_type=MESH
        ).start()

    def wait(ref, sem):
        pltpu.make_async_copy(ref, ref, sem).wait()

    def of(i, n):
        return pl.ds(pl.multiple_of(i, n), n)

    barrier = pltpu.get_barrier_semaphore()
    greet = [partner]
    for d in (1, 3):
        for core in (0, 1):
            greet.append((lax.rem(z + d, 4), x, core, y))
            greet.append((z, lax.rem(x + d, 4), core, y))
        greet.append(ydev(d))
    for dev in greet:
        pl.semaphore_signal(barrier, inc=1, device_id=dev, device_id_type=MESH)
    loads = [
        pltpu.make_async_copy(src, dst, load_sem.at[i])
        for i, (src, dst) in enumerate(
            ((ascale_hbm, ascale), (acts_hbm, acts_raw), (gscale_hbm, gscale), (grads_hbm, grads_raw))
        )
    ]
    for load in loads:
        load.start()

    loads[0].wait()
    for r in range(ROWS // 128):
        wide[:, r * 128 : (r + 1) * 128] = jnp.broadcast_to(
            ascale[:, r : r + 1].astype(F32), (2, 128)
        )
    loads[1].wait()

    def scale_step(i, _):
        dst = pl.ds(pl.multiple_of(i * 512, 512), 512)
        for which, put in ((1 - c, 0), (c, 1)):
            cols = pl.ds(pl.multiple_of(which * HALF + i * 512, 512), 512)
            for blk in range(2):
                v = (acts_raw[blk, :, cols].astype(F32) * wide[blk : blk + 1, cols]).astype(BF)
                v = v.reshape(2, 64, 512)
                rows = pl.ds(2 * blk, 2)
                if put:
                    A[0, c, rows, :, dst] = v
                else:
                    S[rows, :, dst] = v
        return 0

    lax.fori_loop(0, HALF // 512, scale_step, 0)

    def turn(i, _):
        cols = pl.ds(pl.multiple_of(i * 512, 512), 512)
        for blk in range(2):
            v = grads_raw[blk, :, cols].astype(F32) * gscale[blk : blk + 1, cols].astype(F32)
            GO[cols, of(c * TOK + blk * 128, 128)] = v.T.astype(BF)
        return 0

    pl.semaphore_wait(barrier, len(greet))

    far = lax.rem(y + 2, 4)
    last_tile = pl.ds(HALF - TILE, TILE)
    groups = (
        (pl.ds(0, TILE), y),
        (pl.ds(TILE, 2 * TILE), y),
        (pl.ds(3 * TILE, HALF - 3 * TILE), y),
        (last_tile, far),
    )
    pieces = (pl.ds(0, TILE), pl.ds(TILE, HALF - TILE))
    def q_own(g, k):
        cols, q = groups[g]
        e = 3 * (g // 3)
        who = c + k * (1 - 2 * c)
        src = A.at[0, who, q, :, cols]
        send(src, A.at[2, who, q, :, cols], q_s.at[e, k], q_r.at[g, 0, who], gdev(1))
        send(src, A.at[1, who, q, :, cols], q_s.at[e + 1, k], q_r.at[g, 1, who], gdev(3))

    def first_group():
        cols, q = groups[0]
        q_own(0, 0)
        src = S.at[q, :, cols]
        send(src, A.at[2, c, q, :, cols], q_s.at[0, 1], q_r.at[0, 0, c], rdev(1, 1 - c))
        send(src, A.at[1, c, q, :, cols], q_s.at[1, 1], q_r.at[0, 1, c], rdev(3, 1 - c))

    def q_relay(g):
        cols, q = groups[g]
        e = 3 * (g // 3) + 2
        wait(A.at[2, 0, q, :, cols], q_r.at[g, 0, 0])
        send(A.at[2, 0, q, :, cols], A.at[3, 0, q, :, cols], q_s.at[e, 0], q_r.at[g, 2, 0], gdev(1))
        wait(A.at[1, 1, q, :, cols], q_r.at[g, 1, 1])
        send(A.at[1, 1, q, :, cols], A.at[3, 1, q, :, cols], q_s.at[e, 1], q_r.at[g, 2, 1], gdev(3))

    def q_near(g):
        cols, q = groups[g]
        wait(A.at[2, 1, q, :, cols], q_r.at[g, 0, 1])
        wait(A.at[1, 0, q, :, cols], q_r.at[g, 1, 0])

    def q_far(g):
        cols, q = groups[g]
        wait(A.at[3, 0, q, :, cols], q_r.at[g, 2, 0])
        wait(A.at[3, 1, q, :, cols], q_r.at[g, 2, 1])

    def q_drain():
        for i in range(3):
            for k in range(2):
                wait(A.at[0, 0, y], q_s.at[i, k])
                wait(A.at[0, 0, y, :, last_tile], q_s.at[3 + i, k])

    def tile(t):
        return pl.ds(pl.multiple_of(t * TILE, TILE), TILE)

    parts = (pl.ds(1, 2), pl.ds(3, 1))
    both = pl.ds(0, 2)
    below = lax.rem(y + 3, 4)
    above = lax.rem(y + 1, 4)

    def y_own(u, i):
        v = A.at[parts[i], both, y, :, tile(u)]
        send(v, v, y_s.at[i, 0], y_r.at[u, 0], ydev(1))
        send(v, v, y_s.at[i, 1], y_r.at[u, 1], ydev(3))

    three = pl.ds(1, 3)

    def y_relay(u):
        wait(A.at[three, both, below, :, tile(u)], y_r.at[u, 0])
        v = A.at[three, 0, below, :, tile(u)]
        send(v, v, y_s.at[2, 0], y_r.at[u, 2], ydev(1))
        wait(A.at[three, both, above, :, tile(u)], y_r.at[u, 1])
        v = A.at[three, 1, above, :, tile(u)]
        send(v, v, y_s.at[2, 1], y_r.at[u, 2], ydev(3))

    def y_done(u):
        wait(A.at[three, both, far, :, tile(u)], y_r.at[u, 2])

    def y_drain():
        for k in range(2):
            for i in range(2):
                wait(A.at[parts[i], both, y], y_s.at[i, k])
            wait(A.at[three, 0, y, :, pl.ds(0, HALF - TILE)], y_s.at[2, k])

    def y_near(u):
        wait(A.at[three, both, below, :, tile(u)], y_r.at[u, 0])
        wait(A.at[three, both, above, :, tile(u)], y_r.at[u, 1])

    first_group()
    for i in range(2):
        send(S.at[:, :, pieces[i]], A.at[0, c, :, :, pieces[i]], pair_s.at[i], pair_r.at[i], partner)
    q_own(1, 0)
    q_own(2, 0)
    wait(A.at[0, 1 - c, :, :, pieces[0]], pair_r.at[0])

    loads[2].wait()
    loads[3].wait()
    lax.fori_loop(0, 10, turn, 0)
    half = GO.at[:, of(c * TOK, TOK)]
    send(half, half, pair_s.at[2], pair_r.at[2], partner)
    wait(A.at[0, 1 - c, :, :, pieces[1]], pair_r.at[1])
    q_own(1, 1)
    q_own(2, 1)
    q_relay(0)
    q_near(0)
    y_own(0, 0)
    q_relay(1)

    def block(da, p, part, n):
        aa = lax.rem(a + da, 4)
        bb = lax.rem(b + B_OFF[p], 4)
        start = (bb * 4 + aa + c * 3 * (aa - bb)) * BLK + part * OWN
        return pl.ds(pl.multiple_of(start, OWN), n)

    wait(GO.at[:, of((1 - c) * TOK, TOK)], pair_r.at[2])
    own_copies = [
        pltpu.make_async_copy(GO.at[block(0, p, 0, BLK)], G.at[p, :, pl.ds(0, 512)], own_sem.at[p])
        for p in range(4)
    ]

    def hop(p):
        send(GO.at[block(2, p, 0, OWN)], RB.at[0, p], hop_s.at[0], hop_r.at[0, p], gdev(1))
        send(GO.at[block(2, p, 1, OWN)], RB.at[1, p], hop_s.at[1], hop_r.at[1, p], gdev(3))

    slot1, slot2, slot3 = pl.ds(512, 512), pl.ds(1024, 512), pl.ds(1536, 512)
    first, second = pl.ds(0, OWN), pl.ds(OWN, OWN)

    def near(p):
        send(GO.at[block(1, p, 0, BLK)], G.at[p, :, slot2], nbr_s.at[0], blk_r.at[p], gdev(1))
        send(GO.at[block(3, p, 0, BLK)], G.at[p, :, slot1], nbr_s.at[1], blk_r.at[p], gdev(3))

    def hop_relay(p):
        wait(RB.at[0, p], hop_r.at[0, p])
        send(RB.at[0, p], G.at[p, first, slot3], rel_s.at[0], blk_r.at[p], gdev(1))
        wait(RB.at[1, p], hop_r.at[1, p])
        send(RB.at[1, p], G.at[p, second, slot3], rel_s.at[1], blk_r.at[p], gdev(3))

    def block_done(p):
        own_copies[p].wait()
        wait(G.at[p, :, pl.ds(512, 1536)], blk_r.at[p])

    hop(0)
    q_near(1)
    y_own(1, 0)
    q_far(0)
    y_own(0, 1)
    for cp in own_copies:
        cp.start()
    q_far(1)
    y_own(1, 1)
    q_relay(2)
    for p in range(1, 4):
        hop(p)
    near(0)

    def y_both(u):
        y_own(u, 0)
        y_own(u, 1)

    y_both(2)
    y_relay(0)
    q_near(2)
    q_far(2)
    y_both(3)
    hop_relay(0)
    near(1)
    hop_relay(1)
    near(2)
    y_relay(1)
    hop_relay(2)
    near(3)
    hop_relay(3)
    q_own(3, 0)
    q_own(3, 1)
    y_relay(2)
    y_both(4)
    y_relay(3)
    y_both(5)
    y_relay(4)
    y_both(6)

    for p in range(3):
        block_done(p)
    acc[...] = jnp.zeros_like(acc)

    def out_tile(h, t):
        return pl.ds(pl.multiple_of(h * HALF + t * TILE, TILE), TILE)

    def product(p, n, t):
        acts = A[:, :, :, :, tile(t)].reshape(4 * 512, TILE)
        left = G[p : p + n].reshape(n * BLK, 2048)
        return jnp.dot(left, acts, preferred_element_type=F32).astype(BF).reshape(n, BLK, TILE)

    def reduce_send(d, part, core, t):
        src = PB.at[1 + d, pl.ds(part * OWN, OWN), tile(t)]
        send(src, RF.at[d, :, out_tile(c, t)], rf_s.at[d, core], fin_r.at[t], rdev(1 + 2 * d, core))

    def add_send(t):
        for d in (0, 1):
            wait(H.at[d, :, tile(t)], rh_r.at[d, t])
            rows = pl.ds(d * OWN, OWN)
            total = PB[1 + d, rows, tile(t)].astype(F32) + H[d, :, tile(t)].astype(F32)
            PB[1 + d, rows, tile(t)] = total.astype(BF)
            reduce_send(d, d, d, t)

    keep = of(c * OWN, OWN)
    give = of((1 - c) * OWN, OWN)

    def own_block(t):
        PB[3, :, tile(t)] = product(3, 1, t)[0]
        send(PB.at[3, give, tile(t)], PP.at[:, out_tile(c, t)], pp_s.at[0], fin_r.at[t], partner)
        PP[:, out_tile(c, t)] = PB[3, keep, tile(t)]

    def copy_out(h, t):
        cols = out_tile(h, t)
        return pltpu.make_async_copy(GR.at[:, cols], grad_out.at[:, cols], out_sem.at[0])

    def finish(t):
        wait(RF.at[0, :, pl.ds(0, 5 * TILE)], fin_r.at[t])
        for h in (0, 1):
            cols = out_tile(h, t)
            g = PP[:, cols].astype(F32) + RF[0, :, cols].astype(F32) + RF[1, :, cols].astype(F32)
            GR[:, cols] = g
            copy_out(h, t).start()
            sq = jnp.sum((g * g).reshape(OWN // 8, 8, TILE), axis=0)
            acc[...] += sq[:, :128] + sq[:, 128:]

    def relay_and_send(u):
        y_relay(u)
        if u + 2 < STEPS:
            y_both(u + 2)

    def last_arrivals():
        q_near(3)
        q_far(3)
        y_near(STEPS - 1)

    def step(t, _):
        pl.when(t < STEPS - 1)(functools.partial(y_done, t))
        pl.when(t == STEPS - 1)(last_arrivals)
        PB[0:3, :, tile(t)] = product(0, 3, t)
        send(PB.at[0, first, tile(t)], H.at[0, :, tile(t)], rh_s.at[0], rh_r.at[0, t], rdev(1, c))
        send(PB.at[0, second, tile(t)], H.at[1, :, tile(t)], rh_s.at[1], rh_r.at[1, t], rdev(3, c))
        reduce_send(0, 1, 1, t)
        reduce_send(1, 0, 0, t)

        for at, u in ((1, 5), (3, 6)):
            pl.when(t == at)(functools.partial(relay_and_send, u))
        pl.when(t == 3)(functools.partial(q_relay, 3))

        pl.when(t >= 1)(functools.partial(add_send, t - 1))
        pl.when(t == 2)(functools.partial(block_done, 3))
        pl.when(t == 2)(functools.partial(own_block, t - 2))
        pl.when(t == 3)(functools.partial(own_block, t - 2))
        pl.when(t >= 3)(functools.partial(own_block, t - 1))
        pl.when(t >= 3)(functools.partial(finish, t - 3))
        return 0

    lax.fori_loop(0, STEPS, step, 0)
    own_block(STEPS - 1)
    add_send(STEPS - 1)

    def last(t, _):
        finish(t)
        return 0

    lax.fori_loop(STEPS - 3, STEPS, last, 0)

    me = ((z * 4 + x) * 2 + c) * 4 + y
    NS[0] = jnp.sum(acc[...], axis=0, keepdims=True)
    N1[me] = NS[0]

    def tell(dz, far, i, _):
        dev = (
            lax.rem(z + dz, 4),
            lax.rem(x + far + lax.div(i, 8), 4),
            lax.rem(c + lax.rem(lax.div(i, 4), 2), 2),
            lax.rem(y + far + lax.rem(i, 4), 4),
        )
        send(NS.at[0], N1.at[me], n_s.at[0], n_r.at[0], dev)
        return 0

    for dz in (2, 1, 3):
        lax.fori_loop(0, 32, functools.partial(tell, dz, 2), 0)
    lax.fori_loop(1, 32, functools.partial(tell, 0, 0), 0)

    for i in range(2):
        wait(S.at[:, :, pieces[i]], pair_s.at[i])
    wait(half, pair_s.at[2])
    q_drain()
    for d in (0, 1):
        wait(RB.at[d], hop_s.at[d])
        wait(RB.at[d], rel_s.at[d])
        wait(G.at[:, :, slot1], nbr_s.at[d])
        wait(H.at[d], rh_s.at[d])
        for core in (0, 1):
            wait(H.at[d], rf_s.at[d, core])
    wait(H.at[0], pp_s.at[0])
    wait(GR, out_sem.at[0])
    y_drain()
    others = N1.at[pl.ds(0, 127)]
    wait(others, n_r.at[0])
    total = jnp.sum(jnp.sum(N1[...], axis=0), keepdims=True)
    limit = clip_rms * jnp.sqrt(jnp.full((1, 1), FF * ROWS, F32))
    factor_out[...] = jnp.broadcast_to(jnp.minimum(1.0, limit / jnp.sqrt(total)), (8, 128))
    wait(others, n_s.at[0])


def adam_kernel(factor, grad, moment, second, master, nm_out, ns_out, nw_out, w_out, nm, ns, nw, w, sems):
    f = factor[0:1, 0:1]
    pairs = ((nm, nm_out), (ns, ns_out), (nw, nw_out), (w, w_out))

    def step(i, _):
        rows = pl.ds(pl.multiple_of(i * 16, 16), 16)
        clipped = f * grad[rows, :]
        new_moment = beta_first * moment[rows, :] + (1.0 - beta_first) * clipped
        new_second = beta_second * second[rows, :] + (1.0 - beta_second) * clipped * clipped
        new_master = master[rows, :] - learn_rate * new_moment / (jnp.sqrt(new_second) + adam_eps)
        nm[rows, :] = new_moment
        ns[rows, :] = new_second
        nw[rows, :] = new_master
        w[rows, :] = new_master.astype(BF)
        for k, (src, dst) in enumerate(pairs):
            pltpu.make_async_copy(src.at[rows], dst.at[rows], sems.at[k]).start()
        return 0

    lax.fori_loop(0, OWN // 16, step, 0)
    for k, (src, dst) in enumerate(pairs):
        pltpu.make_async_copy(src, dst, sems.at[k]).wait()


def adam(factor, grad, moment, second, master):
    vmem = pltpu.VMEM
    shape = (OWN, ROWS)
    kinds = (F32, F32, F32, BF)
    return pl.pallas_call(
        adam_kernel,
        out_shape=tuple(jax.ShapeDtypeStruct(shape, kind) for kind in kinds),
        in_specs=[pl.BlockSpec(memory_space=vmem)] * 5,
        out_specs=tuple(pl.BlockSpec(memory_space=pltpu.HBM) for _ in kinds),
        scratch_shapes=[vmem(shape, kind) for kind in kinds] + [pltpu.SemaphoreType.DMA((4,))],
        compiler_params=pltpu.CompilerParams(vmem_limit_bytes=24 * 1024 * 1024),
        cost_estimate=pl.CostEstimate(flops=20 * OWN * ROWS, bytes_accessed=30 * OWN * ROWS, transcendentals=OWN * ROWS),
        name="adam",
    )(factor, grad, moment, second, master)


def owned_gradient(activations, out_grads, act_scale, grad_scale):
    dma = pltpu.SemaphoreType.DMA
    vmem = pltpu.VMEM
    scratch = [
        vmem((2, 128, ROWS), BF),
        vmem((2, 128, 5120), BF),
        vmem((2, ROWS // 128), BF),
        vmem((2, 5120), BF),
        vmem((2, ROWS), F32),
        vmem((4, 2, 4, 64, HALF), BF),
        vmem((4, 64, HALF), BF),
        vmem((5120, 512), BF),
        vmem((4, BLK, 2048), BF),
        vmem((2, 4, OWN, 512), BF),
        vmem((4, BLK, HALF), BF),
        vmem((2, OWN, HALF), BF),
        vmem((2, OWN, ROWS), BF),
        vmem((OWN, ROWS), BF),
        vmem((OWN, ROWS), F32),
        vmem((8, 128), F32),
        vmem((1, 1, 128), F32),
        vmem((128, 1, 128), F32),
        dma((4,)),
        dma((4,)),
        dma((3,)), dma((3,)),
        dma((6, 2)), dma((4, 3, 2)),
        dma((3, 2)), dma((STEPS, 3)),
        dma((2,)), dma((2, 4)),
        dma((2,)), dma((2,)), dma((4,)),
        dma((2,)), dma((2, STEPS)),
        dma((2, 2)), dma((1,)), dma((STEPS,)),
        dma((1,)),
        dma((1,)), dma((1,)),
    ]
    return pl.pallas_call(
        kernel,
        out_shape=(
            jax.ShapeDtypeStruct((OWN, ROWS), F32),
            jax.ShapeDtypeStruct((8, 128), F32),
        ),
        in_specs=[pl.BlockSpec(memory_space=pltpu.HBM)] * 4,
        out_specs=(pl.BlockSpec(memory_space=pl.ANY), pl.BlockSpec(memory_space=vmem)),
        scratch_shapes=scratch,
        compiler_params=pltpu.CompilerParams(
            collective_id=0, has_side_effects=True, vmem_limit_bytes=46 * 1024 * 1024
        ),
        cost_estimate=pl.CostEstimate(
            flops=2 * 8192 * OWN * ROWS, bytes_accessed=8 * 1024 * 1024, transcendentals=0
        ),
        name="owned_gradient",
    )(*(
        pltpu.with_memory_space_constraint(v, pltpu.HBM)
        for v in (activations, out_grads, act_scale, grad_scale.reshape(2, 5120))
    ))


def per_device(activations, out_grads, act_scale, grad_scale, moment, second, master):
    grad_owned, factors = owned_gradient(activations, out_grads, act_scale, grad_scale)
    return adam(factors, grad_owned, moment, second, master)


def solution(mesh):
    finer = Mesh(
        mesh.devices.reshape(4, 4, 2, mesh.shape["tensor"]), ("dp_0", "dp_1", "dp_2", "tensor")
    )
    in_specs = (
        P(DP, None, None),
        P(DP, None, "tensor"),
        P(DP, None),
        P(DP, None, "tensor"),
        P(TENSOR_DP, None),
        P(TENSOR_DP, None),
        P(TENSOR_DP, None),
    )
    out_specs = (P(TENSOR_DP, None), P(TENSOR_DP, None), P(TENSOR_DP, None), P(TENSOR_DP, None))
    return jax.shard_map(
        per_device, mesh=finer, in_specs=in_specs, out_specs=out_specs, check_vma=False
    )
```

time: 97.1 us -> 87.4 us (0.900)
  other arithmetic: 5.34 us -> 0 us
  Pallas kernels: 91 us -> 85.8 us
    pallas_call x1, Pallas kernels: 91 us -> 82 us  [owned_gradient(): pl.pallas_call(kernel, out_shape=(jax.ShapeDtypeStruct((OWN, ROWS), F32),...]
    convert_element_type x1 -> x0, other arithmetic: 5.34 us -> none  [per_device(): weights = new_master.astype(jnp.bfloat16)]
    pallas_call x0 -> x1, Pallas kernels: none -> 3.85 us  [adam(): pl.pallas_call(adam_kernel, out_shape=tuple((jax.ShapeDtypeStruct(shape,...]
where the time goes in v3:
time: 87.4 us; the launch traced here: 86.5 us
  Pallas kernels  85.8 us (98%)
    pallas_call x1, Pallas kernels, owned_gradient(): pl.pallas_call(kernel, out_shape=(jax.ShapeDtypeStruct((OWN, ROWS), F32),...  82 us
    pallas_call x1, Pallas kernels, adam(): pl.pallas_call(adam_kernel, out_shape=tuple((jax.ShapeDtypeStruct(shape,...  3.85 us

profile of v3, /device:TPU:0, one launch (start us, length us, event | category | flops | bytes accessed | tf_op | source)
XLA Modules:
  0.0 86.5 jit_solution(255854161540950189)
XLA Ops:
  0.6 0.0 copy-start
  0.6 0.0 copy-start.1
  0.7 0.0 copy-start.2
  0.7 82.0 %owned_gradient.1 = (f32[160,4096]{1,0:T(8,128)S(1)}, f32[8,128]{1,0:T(8,128)S(1)}) custom-call(bf16[2,128,4096]{2,1,0:T(8,128)(2,1)} %acts_hbm.1, bf16[2,128,5120]{2,1,0:T(8,128)(2,1)} %grads_hbm.1, bf16[2,32]{1,0:T(2,128)(2,1)} %ascale_hbm.1, bf16[2,5120]{1,0:T(2,128)(2,1)} %bitcast.1), custom_call_target="tpu_custom_call" | custom-call | flops 10737418240 | bytes 8388608 | tf_op jit(solution)/shard_map/owned_gradient/pallas_call | solution.py:499
  82.7 0.0 copy-done
  82.7 0.0 copy-done.1
  82.7 0.0 copy-done.2
  82.7 3.8 %adam.1 = (f32[160,4096]{1,0:T(8,128)}, f32[160,4096]{1,0:T(8,128)}, f32[160,4096]{1,0:T(8,128)}, bf16[160,4096]{1,0:T(8,128)(2,1)}) custom-call(f32[8,128]{1,0:T(8,128)S(1)} %get-tuple-element.6.factor, f32[160,4096]{1,0:T(8,128)S(1)} %get-tuple-element.7.grad, f32[160,4096]{1,0:T(8,128)S(1)} %copy-done, f32[160,4096]{1,0:T(8,128)S(1)} %copy-done.1, ...), custom_call_target="tpu_custom_call" | custom-call | flops 13107200 | bytes 19660800 | tf_op jit(solution)/shard_map/adam/pallas_call | solution.py:453
Async XLA Ops:
  0.6 82.0 %copy-start = (f32[160,4096]{1,0:T(8,128)S(1)}, f32[160,4096]{1,0:T(8,128)}, u32[]{:S(2)}) copy-start(f32[160,4096]{1,0:T(8,128)} %moment.1) | copy-start | bytes 7864324
  0.6 82.0 %copy-start.1 = (f32[160,4096]{1,0:T(8,128)S(1)}, f32[160,4096]{1,0:T(8,128)}, u32[]{:S(2)}) copy-start(f32[160,4096]{1,0:T(8,128)} %second.1) | copy-start | bytes 7864324
  0.7 82.0 %copy-start.2 = (f32[160,4096]{1,0:T(8,128)S(1)}, f32[160,4096]{1,0:T(8,128)}, u32[]{:S(2)}) copy-start(f32[160,4096]{1,0:T(8,128)} %master.1) | copy-start | bytes 7864324

commit v4 on v3

--- a/solution.py
+++ b/solution.py
@@ -120,12 +120,12 @@
     pl.semaphore_wait(barrier, len(greet))
 
     far = lax.rem(y + 2, 4)
-    last_tile = pl.ds(HALF - TILE, TILE)
+    last_tiles = pl.ds(HALF - 2 * TILE, 2 * TILE)
     groups = (
         (pl.ds(0, TILE), y),
         (pl.ds(TILE, 2 * TILE), y),
         (pl.ds(3 * TILE, HALF - 3 * TILE), y),
-        (last_tile, far),
+        (last_tiles, far),
     )
     pieces = (pl.ds(0, TILE), pl.ds(TILE, HALF - TILE))
     def q_own(g, k):
@@ -165,7 +165,7 @@
         for i in range(3):
             for k in range(2):
                 wait(A.at[0, 0, y], q_s.at[i, k])
-                wait(A.at[0, 0, y, :, last_tile], q_s.at[3 + i, k])
+                wait(A.at[0, 0, y, :, last_tiles], q_s.at[3 + i, k])
 
     def tile(t):
         return pl.ds(pl.multiple_of(t * TILE, TILE), TILE)
@@ -197,7 +197,7 @@
         for k in range(2):
             for i in range(2):
                 wait(A.at[parts[i], both, y], y_s.at[i, k])
-            wait(A.at[three, 0, y, :, pl.ds(0, HALF - TILE)], y_s.at[2, k])
+            wait(A.at[three, 0, y, :, pl.ds(0, HALF - 2 * TILE)], y_s.at[2, k])
 
     def y_near(u):
         wait(A.at[three, both, below, :, tile(u)], y_r.at[u, 0])
@@ -257,6 +257,7 @@
         wait(G.at[p, :, pl.ds(512, 1536)], blk_r.at[p])
 
     hop(0)
+    hop(1)
     q_near(1)
     y_own(1, 0)
     q_far(0)
@@ -266,7 +267,7 @@
     q_far(1)
     y_own(1, 1)
     q_relay(2)
-    for p in range(1, 4):
+    for p in range(2, 4):
         hop(p)
     near(0)
 
@@ -350,56 +351,51 @@
     def last_arrivals():
         q_near(3)
         q_far(3)
-        y_near(STEPS - 1)
 
     def step(t, _):
-        pl.when(t < STEPS - 1)(functools.partial(y_done, t))
-        pl.when(t == STEPS - 1)(last_arrivals)
+        pl.when(t < STEPS - 2)(functools.partial(y_done, t))
+        pl.when(t == STEPS - 2)(last_arrivals)
+        pl.when(t >= STEPS - 2)(functools.partial(y_near, t))
         PB[0:3, :, tile(t)] = product(0, 3, t)
         send(PB.at[0, first, tile(t)], H.at[0, :, tile(t)], rh_s.at[0], rh_r.at[0, t], rdev(1, c))
         send(PB.at[0, second, tile(t)], H.at[1, :, tile(t)], rh_s.at[1], rh_r.at[1, t], rdev(3, c))
         reduce_send(0, 1, 1, t)
         reduce_send(1, 0, 0, t)
 
-        for at, u in ((1, 5), (3, 6)):
-            pl.when(t == at)(functools.partial(relay_and_send, u))
+        pl.when(t == 2)(functools.partial(block_done, 3))
+        pl.when(t >= 2)(functools.partial(own_block, t - 2))
+        pl.when(t >= 1)(functools.partial(add_send, t - 1))
+        pl.when(t >= 3)(functools.partial(finish, t - 3))
+        pl.when(t == 1)(functools.partial(relay_and_send, 5))
         pl.when(t == 3)(functools.partial(q_relay, 3))
-
-        pl.when(t >= 1)(functools.partial(add_send, t - 1))
-        pl.when(t == 2)(functools.partial(block_done, 3))
-        pl.when(t == 2)(functools.partial(own_block, t - 2))
-        pl.when(t == 3)(functools.partial(own_block, t - 2))
-        pl.when(t >= 3)(functools.partial(own_block, t - 1))
-        pl.when(t >= 3)(functools.partial(finish, t - 3))
         return 0
 
     lax.fori_loop(0, STEPS, step, 0)
+    own_block(STEPS - 2)
     own_block(STEPS - 1)
+    finish(STEPS - 3)
     add_send(STEPS - 1)
-
-    def last(t, _):
-        finish(t)
-        return 0
-
-    lax.fori_loop(STEPS - 3, STEPS, last, 0)
+    finish(STEPS - 2)
+    finish(STEPS - 1)
 
     me = ((z * 4 + x) * 2 + c) * 4 + y
     NS[0] = jnp.sum(acc[...], axis=0, keepdims=True)
     N1[me] = NS[0]
 
-    def tell(dz, far, i, _):
-        dev = (
-            lax.rem(z + dz, 4),
-            lax.rem(x + far + lax.div(i, 8), 4),
-            lax.rem(c + lax.rem(lax.div(i, 4), 2), 2),
-            lax.rem(y + far + lax.rem(i, 4), 4),
-        )
-        send(NS.at[0], N1.at[me], n_s.at[0], n_r.at[0], dev)
-        return 0
-
-    for dz in (2, 1, 3):
-        lax.fori_loop(0, 32, functools.partial(tell, dz, 2), 0)
-    lax.fori_loop(1, 32, functools.partial(tell, 0, 0), 0)
+    planes = [lax.rem(y + k, 4) for k in (2, 1, 3, 0)]
+
+    def tell(dz, dx):
+        for dc in (1, 0):
+            for dy, plane in zip((2, 1, 3, 0), planes):
+                if dz or dx or dc or dy:
+                    dev = (lax.rem(z + dz, 4), lax.rem(x + dx, 4), lax.rem(c + dc, 2), plane)
+                    send(NS.at[0], N1.at[me], n_s.at[0], n_r.at[0], dev)
+
+    for hops in (4, 3, 2, 1, 0):
+        for dz in (2, 1, 3, 0):
+            for dx in (2, 1, 3, 0):
+                if min(dz, 4 - dz) + min(dx, 4 - dx) == hops:
+                    tell(dz, dx)
 
     for i in range(2):
         wait(S.at[:, :, pieces[i]], pair_s.at[i])

time: 87.4 us -> 83.7 us (0.958)
  Pallas kernels: 85.8 us -> 82.2 us
    pallas_call x1, Pallas kernels: 82 us -> 78.3 us  [owned_gradient(): pl.pallas_call(kernel, out_shape=(jax.ShapeDtypeStruct((OWN, ROWS), F32),...]
where the time goes in v4:
time: 83.7 us; the launch traced here: 82.9 us
  Pallas kernels  82.2 us (98%)
    pallas_call x1, Pallas kernels, owned_gradient(): pl.pallas_call(kernel, out_shape=(jax.ShapeDtypeStruct((OWN, ROWS), F32),...  78.3 us
    pallas_call x1, Pallas kernels, adam(): pl.pallas_call(adam_kernel, out_shape=tuple((jax.ShapeDtypeStruct(shape,...  3.85 us

profile of v4, /device:TPU:0, one launch (start us, length us, event | category | flops | bytes accessed | tf_op | source)
XLA Modules:
  0.0 82.9 jit_solution(9893939321403627801)
XLA Ops:
  0.6 0.0 copy-start
  0.6 0.0 copy-start.1
  0.7 0.0 copy-start.2
  0.7 78.3 %owned_gradient.1 = (f32[160,4096]{1,0:T(8,128)S(1)}, f32[8,128]{1,0:T(8,128)S(1)}) custom-call(bf16[2,128,4096]{2,1,0:T(8,128)(2,1)} %acts_hbm.1, bf16[2,128,5120]{2,1,0:T(8,128)(2,1)} %grads_hbm.1, bf16[2,32]{1,0:T(2,128)(2,1)} %ascale_hbm.1, bf16[2,5120]{1,0:T(2,128)(2,1)} %bitcast.1), custom_call_target="tpu_custom_call" | custom-call | flops 10737418240 | bytes 8388608 | tf_op jit(solution)/shard_map/owned_gradient/pallas_call | solution.py:495
  79.0 0.0 copy-done
  79.0 0.0 copy-done.1
  79.0 0.0 copy-done.2
  79.0 3.8 %adam.1 = (f32[160,4096]{1,0:T(8,128)}, f32[160,4096]{1,0:T(8,128)}, f32[160,4096]{1,0:T(8,128)}, bf16[160,4096]{1,0:T(8,128)(2,1)}) custom-call(f32[8,128]{1,0:T(8,128)S(1)} %get-tuple-element.6.factor, f32[160,4096]{1,0:T(8,128)S(1)} %get-tuple-element.7.grad, f32[160,4096]{1,0:T(8,128)S(1)} %copy-done, f32[160,4096]{1,0:T(8,128)S(1)} %copy-done.1, ...), custom_call_target="tpu_custom_call" | custom-call | flops 13107200 | bytes 19660800 | tf_op jit(solution)/shard_map/adam/pallas_call | solution.py:449
Async XLA Ops:
  0.6 78.4 %copy-start = (f32[160,4096]{1,0:T(8,128)S(1)}, f32[160,4096]{1,0:T(8,128)}, u32[]{:S(2)}) copy-start(f32[160,4096]{1,0:T(8,128)} %moment.1) | copy-start | bytes 7864324
  0.6 78.4 %copy-start.1 = (f32[160,4096]{1,0:T(8,128)S(1)}, f32[160,4096]{1,0:T(8,128)}, u32[]{:S(2)}) copy-start(f32[160,4096]{1,0:T(8,128)} %second.1) | copy-start | bytes 7864324
  0.7 78.4 %copy-start.2 = (f32[160,4096]{1,0:T(8,128)S(1)}, f32[160,4096]{1,0:T(8,128)}, u32[]{:S(2)}) copy-start(f32[160,4096]{1,0:T(8,128)} %master.1) | copy-start | bytes 7864324

commit v5 on v4

--- a/solution.py
+++ b/solution.py
@@ -69,6 +69,15 @@
     def of(i, n):
         return pl.ds(pl.multiple_of(i, n), n)
 
+    loads = [
+        pltpu.make_async_copy(src, dst, load_sem.at[i])
+        for i, (src, dst) in enumerate(
+            ((ascale_hbm, ascale), (acts_hbm, acts_raw), (gscale_hbm, gscale), (grads_hbm, grads_raw))
+        )
+    ]
+    for k in (1, 0, 3, 2):
+        loads[k].start()
+
     barrier = pltpu.get_barrier_semaphore()
     greet = [partner]
     for d in (1, 3):
@@ -78,15 +87,6 @@
         greet.append(ydev(d))
     for dev in greet:
         pl.semaphore_signal(barrier, inc=1, device_id=dev, device_id_type=MESH)
-    loads = [
-        pltpu.make_async_copy(src, dst, load_sem.at[i])
-        for i, (src, dst) in enumerate(
-            ((ascale_hbm, ascale), (acts_hbm, acts_raw), (gscale_hbm, gscale), (grads_hbm, grads_raw))
-        )
-    ]
-    for load in loads:
-        load.start()
-
     loads[0].wait()
     for r in range(ROWS // 128):
         wide[:, r * 128 : (r + 1) * 128] = jnp.broadcast_to(
@@ -178,20 +178,19 @@
     def y_own(u, i):
         v = A.at[parts[i], both, y, :, tile(u)]
         send(v, v, y_s.at[i, 0], y_r.at[u, 0], ydev(1))
-        send(v, v, y_s.at[i, 1], y_r.at[u, 1], ydev(3))
+        send(v, v, y_s.at[i, 1], y_r.at[u, 0], ydev(3))
 
     three = pl.ds(1, 3)
 
     def y_relay(u):
-        wait(A.at[three, both, below, :, tile(u)], y_r.at[u, 0])
+        y_near(u)
         v = A.at[three, 0, below, :, tile(u)]
-        send(v, v, y_s.at[2, 0], y_r.at[u, 2], ydev(1))
-        wait(A.at[three, both, above, :, tile(u)], y_r.at[u, 1])
+        send(v, v, y_s.at[2, 0], y_r.at[u, 1], ydev(1))
         v = A.at[three, 1, above, :, tile(u)]
-        send(v, v, y_s.at[2, 1], y_r.at[u, 2], ydev(3))
+        send(v, v, y_s.at[2, 1], y_r.at[u, 1], ydev(3))
 
     def y_done(u):
-        wait(A.at[three, both, far, :, tile(u)], y_r.at[u, 2])
+        wait(A.at[three, both, far, :, tile(u)], y_r.at[u, 1])
 
     def y_drain():
         for k in range(2):
@@ -200,8 +199,7 @@
             wait(A.at[three, 0, y, :, pl.ds(0, HALF - 2 * TILE)], y_s.at[2, k])
 
     def y_near(u):
-        wait(A.at[three, both, below, :, tile(u)], y_r.at[u, 0])
-        wait(A.at[three, both, above, :, tile(u)], y_r.at[u, 1])
+        wait(A.at[three, both, both, :, tile(u)], y_r.at[u, 0])
 
     first_group()
     for i in range(2):
@@ -314,8 +312,8 @@
         send(src, RF.at[d, :, out_tile(c, t)], rf_s.at[d, core], fin_r.at[t], rdev(1 + 2 * d, core))
 
     def add_send(t):
+        wait(H.at[:, :, tile(t)], rh_r.at[t])
         for d in (0, 1):
-            wait(H.at[d, :, tile(t)], rh_r.at[d, t])
             rows = pl.ds(d * OWN, OWN)
             total = PB[1 + d, rows, tile(t)].astype(F32) + H[d, :, tile(t)].astype(F32)
             PB[1 + d, rows, tile(t)] = total.astype(BF)
@@ -357,8 +355,8 @@
         pl.when(t == STEPS - 2)(last_arrivals)
         pl.when(t >= STEPS - 2)(functools.partial(y_near, t))
         PB[0:3, :, tile(t)] = product(0, 3, t)
-        send(PB.at[0, first, tile(t)], H.at[0, :, tile(t)], rh_s.at[0], rh_r.at[0, t], rdev(1, c))
-        send(PB.at[0, second, tile(t)], H.at[1, :, tile(t)], rh_s.at[1], rh_r.at[1, t], rdev(3, c))
+        send(PB.at[0, first, tile(t)], H.at[0, :, tile(t)], rh_s.at[0], rh_r.at[t], rdev(1, c))
+        send(PB.at[0, second, tile(t)], H.at[1, :, tile(t)], rh_s.at[1], rh_r.at[t], rdev(3, c))
         reduce_send(0, 1, 1, t)
         reduce_send(1, 0, 0, t)
 
@@ -484,10 +482,10 @@
         dma((4,)),
         dma((3,)), dma((3,)),
         dma((6, 2)), dma((4, 3, 2)),
-        dma((3, 2)), dma((STEPS, 3)),
+        dma((3, 2)), dma((STEPS, 2)),
         dma((2,)), dma((2, 4)),
         dma((2,)), dma((2,)), dma((4,)),
-        dma((2,)), dma((2, STEPS)),
+        dma((2,)), dma((STEPS,)),
         dma((2, 2)), dma((1,)), dma((STEPS,)),
         dma((1,)),
         dma((1,)), dma((1,)),

time: 83.7 us -> 83.6 us (level)
  no operation moved by 1% of the time
where the time goes in v5:
time: 83.6 us; the launch traced here: 82.8 us
  Pallas kernels  82.1 us (98%)
    pallas_call x1, Pallas kernels, owned_gradient(): pl.pallas_call(kernel, out_shape=(jax.ShapeDtypeStruct((OWN, ROWS), F32),...  78.3 us
    pallas_call x1, Pallas kernels, adam(): pl.pallas_call(adam_kernel, out_shape=tuple((jax.ShapeDtypeStruct(shape,...  3.85 us

profile of v5, /device:TPU:0, one launch (start us, length us, event | category | flops | bytes accessed | tf_op | source)
XLA Modules:
  0.0 82.8 jit_solution(3665421981197265819)
XLA Ops:
  0.6 0.0 copy-start
  0.6 0.0 copy-start.1
  0.7 0.0 copy-start.2
  0.7 78.3 %owned_gradient.1 = (f32[160,4096]{1,0:T(8,128)S(1)}, f32[8,128]{1,0:T(8,128)S(1)}) custom-call(bf16[2,128,4096]{2,1,0:T(8,128)(2,1)} %acts_hbm.1, bf16[2,128,5120]{2,1,0:T(8,128)(2,1)} %grads_hbm.1, bf16[2,32]{1,0:T(2,128)(2,1)} %ascale_hbm.1, bf16[2,5120]{1,0:T(2,128)(2,1)} %bitcast.1), custom_call_target="tpu_custom_call" | custom-call | flops 10737418240 | bytes 8388608 | tf_op jit(solution)/shard_map/owned_gradient/pallas_call | solution.py:493
  79.0 0.0 copy-done
  79.0 0.0 copy-done.1
  79.0 0.0 copy-done.2
  79.0 3.8 %adam.1 = (f32[160,4096]{1,0:T(8,128)}, f32[160,4096]{1,0:T(8,128)}, f32[160,4096]{1,0:T(8,128)}, bf16[160,4096]{1,0:T(8,128)(2,1)}) custom-call(f32[8,128]{1,0:T(8,128)S(1)} %get-tuple-element.6.factor, f32[160,4096]{1,0:T(8,128)S(1)} %get-tuple-element.7.grad, f32[160,4096]{1,0:T(8,128)S(1)} %copy-done, f32[160,4096]{1,0:T(8,128)S(1)} %copy-done.1, ...), custom_call_target="tpu_custom_call" | custom-call | flops 13107200 | bytes 19660800 | tf_op jit(solution)/shard_map/adam/pallas_call | solution.py:447
Async XLA Ops:
  0.6 78.3 %copy-start = (f32[160,4096]{1,0:T(8,128)S(1)}, f32[160,4096]{1,0:T(8,128)}, u32[]{:S(2)}) copy-start(f32[160,4096]{1,0:T(8,128)} %moment.1) | copy-start | bytes 7864324
  0.6 78.3 %copy-start.1 = (f32[160,4096]{1,0:T(8,128)S(1)}, f32[160,4096]{1,0:T(8,128)}, u32[]{:S(2)}) copy-start(f32[160,4096]{1,0:T(8,128)} %second.1) | copy-start | bytes 7864324
  0.7 78.3 %copy-start.2 = (f32[160,4096]{1,0:T(8,128)S(1)}, f32[160,4096]{1,0:T(8,128)}, u32[]{:S(2)}) copy-start(f32[160,4096]{1,0:T(8,128)} %master.1) | copy-start | bytes 7864324
